TPU v7x, 32 devices: a whole 2x2x4 slice. The times are simulated.
32 devices in a mesh: seq: 8 (over z, x), head: 4 (over y, core).
Axes of the slice: x: 2, y: 2, z: 4, core: 2. Of those that a mesh axis runs over, the one named last changes fastest.
Arguments:
- queries: bfloat16 [2048, 4096], P('seq', 'head'), may hold values from -48 to 48
- key_rows: bfloat16 [2048, 4096], P('seq', 'head'), may hold values from -4 to 4
- value_rows: bfloat16 [2048, 4096], P('seq', 'head'), may hold values from -6 to 6
- out_grad: bfloat16 [2048, 2048], P('seq', 'head'), may hold values from -6 to 6
- out_proj: bfloat16 [4096, 2048], P('head'), may hold values from -0.125 to 0.125
- section_table: int32 [32, 3], P('head'), may hold values 0 or 1
- block_active: int32 [8, 3], P('seq'), may hold values 0 or 1
Outputs:
- query_grad: bfloat16 [2048, 4096], P('seq', 'head')
- key_grad: bfloat16 [2048, 4096], P('seq', 'head')
- value_grad: bfloat16 [2048, 4096], P('seq', 'head')
All inputs are finite; a program needn't handle non-finite values.
Results may differ from a plain program's by a relative error of at most 0.008.
Values may be sent and summed in bfloat16 or wider, within the bound.
A program may use at most 64 MiB of HBM per device.

v0:
```python
import functools
import math

import jax
import jax.numpy as jnp
from jax import lax
from jax.experimental import pallas as pl
from jax.experimental.pallas import tpu as pltpu
from jax.sharding import PartitionSpec as P

HDIM = 128
SECTIONS = 3
AHEAD = 2
MESH = pl.DeviceIdType.MESH
BF16 = jnp.bfloat16
F32 = jnp.float32


def dot(a, b, dims):
    return lax.dot_general(a, b, (dims, ((), ())), preferred_element_type=F32)


def kernel(
    count,
    lanes,
    q_ref,
    k_hbm,
    v_hbm,
    og_hbm,
    proj_hbm,
    table_ref,
    active_ref,
    dq_hbm,
    dk_hbm,
    dv_hbm,
    kv,
    reach,
    term,
    back,
    own,
    og,
    proj,
    local_sem,
    load_sem,
    og_send,
    og_recv,
    fwd_send,
    fwd_recv,
    bwd_send,
    bwd_recv,
    result,
    out_sem,
):
    heads, _, rows, _ = kv.shape
    width = og.shape[2]
    scale = 1.0 / math.sqrt(HDIM)
    quarter, eighth = count // 4, count // 8
    me = lax.axis_index("seq")
    lane = lax.axis_index("head")
    odd = (me // eighth) % 2 == 1
    even = jnp.logical_not(odd)
    up, down = me + quarter, me - quarter
    pair = jnp.where(odd, me - eighth, me + eighth)
    has_up, has_down = me < count - quarter, me >= quarter
    has_far = me >= 2 * quarter
    has_both = jnp.logical_and(has_up, has_down)
    odd_or_down = jnp.logical_or(odd, has_down)
    even_or_down = jnp.logical_or(even, has_down)
    twin = jnp.where(lane % 2 == 1, lane - 1, lane + 1)

    def cols(c):
        return pl.ds(pl.multiple_of(c * HDIM, HDIM), HDIM)

    def remote(src, dst, send, recv, axis, target):
        return pltpu.make_async_remote_copy(
            src_ref=src,
            dst_ref=dst,
            send_sem=send,
            recv_sem=recv,
            device_id={axis: target},
            device_id_type=MESH,
        )

    def fwd(kind, src, c, j, target):
        return remote(
            src.at[c, j],
            reach.at[kind, c, j],
            fwd_send.at[kind, j, c],
            fwd_recv.at[kind, j, c],
            "seq",
            target,
        )

    def bwd(kind, c, j, target):
        return remote(
            term.at[kind, c, j],
            back.at[kind, c, j],
            bwd_send.at[kind, j, c],
            bwd_recv.at[kind, j, c],
            "seq",
            target,
        )

    def load_kv(c):
        return [
            pltpu.make_async_copy(src.at[:, cols(c)], kv.at[c, j], local_sem.at[j, c])
            for j, src in enumerate((k_hbm, v_hbm))
        ]

    def write(index, c):
        target = (dq_hbm, dk_hbm, dv_hbm)[index]
        return pltpu.make_async_copy(
            result.at[index, c], target.at[:, cols(c)], out_sem.at[index, c]
        )

    load_og = pltpu.make_async_copy(og_hbm, og.at[lane], load_sem.at[0])
    load_proj = pltpu.make_async_copy(proj_hbm, proj, load_sem.at[1])
    load_og.start()

    @pl.loop(0, heads)
    def _(c):
        for copy in load_kv(c):
            copy.start()

    load_proj.start()

    barrier = pltpu.get_barrier_semaphore()
    peers = [lax.rem(lane + 2 * j, lanes) for j in range(1, lanes // 2)]
    for peer in [twin] + peers:
        pl.semaphore_signal(barrier, inc=1, device_id={"head": peer}, device_id_type=MESH)
    pl.semaphore_signal(barrier, inc=1, device_id={"seq": pair}, device_id_type=MESH)

    @pl.when(has_up)
    def _():
        pl.semaphore_signal(barrier, inc=1, device_id={"seq": up}, device_id_type=MESH)

    @pl.when(has_down)
    def _():
        pl.semaphore_signal(barrier, inc=1, device_id={"seq": down}, device_id_type=MESH)

    pl.semaphore_wait(
        barrier, 2 + len(peers) + has_up.astype(jnp.int32) + has_down.astype(jnp.int32)
    )

    def send_own(c):
        for j, copy in enumerate(load_kv(c)):
            copy.wait()

            @pl.when(has_up)
            def _():
                fwd(1, kv, c, j, up).start()

            @pl.when(even)
            def _():
                fwd(2, kv, c, j, pair).start()

    def forward(c):
        for j in range(2):

            @pl.when(has_down)
            def _():
                fwd(1, kv, c, j, up).wait_recv()

            @pl.when(has_both)
            def _():
                fwd(0, reach.at[1], c, j, up).start()

            @pl.when(jnp.logical_and(odd, has_down))
            def _():
                fwd(2, reach.at[1], c, j, pair).start()

        @pl.when(c + AHEAD < heads)
        def _():
            send_own(c + AHEAD)

    def og_peer(index, slot, target):
        return remote(
            og.at[slot], og.at[slot], og_send.at[index], og_recv.at[slot], "head", target
        )

    load_og.wait()
    for j, peer in enumerate(peers):
        og_peer(1 + j, lane, peer).start()
    og_peer(0, lane, twin).start()
    for c in range(AHEAD):
        send_own(jnp.int32(c))

    for present, buffer in (
        (has_far, reach.at[0]),
        (has_down, reach.at[1]),
        (odd_or_down, reach.at[2]),
        (has_both, back.at[0]),
        (has_up, back.at[1]),
        (even_or_down, back.at[2]),
    ):

        @pl.when(jnp.logical_not(present))
        def _():
            @pl.loop(0, heads)
            def _(c):
                buffer[c] = jnp.zeros(buffer.shape[1:], BF16)

    forward(jnp.int32(0))
    for j, peer in enumerate(peers):
        og_peer(1 + j, peer, lane).wait_recv()
        og_peer(len(peers) + 1 + j, peer, twin).start()
    load_proj.wait()
    og_peer(0, twin, lane).wait_recv()
    for j in range(len(peers)):
        og_peer(len(peers) + 1 + j, lax.rem(twin + 2 * (j + 1), lanes), lane).wait_recv()

    key_index = lax.broadcasted_iota(jnp.int32, (rows, rows), 0)
    query_index = lax.broadcasted_iota(jnp.int32, (rows, rows), 1)

    def compute(c):
        grad = sum(
            dot(og[p], proj[cols(c), p * width : (p + 1) * width], ((1,), (1,)))
            for p in range(lanes)
        ).astype(BF16)
        query = q_ref[:, cols(c)]

        def key_of(k):
            return reach[k - 1, c, 0] if k else kv[c, 0]

        def logits_of(k):
            raw = dot(key_of(k), query, ((1,), (1,))) * scale
            if k == 0:
                return jnp.where(key_index <= query_index, raw, -1e30)
            usable = jnp.logical_and(
                table_ref[k - 1, c] * active_ref[0, k - 1] > 0, me >= count // 2**k
            )
            return raw + jnp.where(usable, 0.0, -1e30).astype(F32)

        def prob_grad_of(k):
            value = reach[k - 1, c, 1] if k else kv[c, 1]
            return dot(value, grad, ((1,), (1,)))

        logits, prob_grads = {}, {}
        for k in (0, 2):
            logits[k], prob_grads[k] = logits_of(k), prob_grad_of(k)
        for j in range(2):

            @pl.when(odd_or_down)
            def _():
                fwd(2, kv, c, j, pair).wait_recv()

        logits[3], prob_grads[3] = logits_of(3), prob_grad_of(3)
        for j in range(2):

            @pl.when(has_far)
            def _():
                fwd(0, kv, c, j, up).wait_recv()

        logits[1], prob_grads[1] = logits_of(1), prob_grad_of(1)
        sets = range(SECTIONS + 1)
        top = functools.reduce(
            jnp.maximum, [jnp.max(logits[k], axis=0, keepdims=True) for k in sets]
        )
        exps = [jnp.exp(logits[k] - top) for k in sets]
        inverse = 1.0 / sum(jnp.sum(x, axis=0, keepdims=True) for x in exps)
        probs = [x * inverse for x in exps]
        weights = [x.astype(BF16) for x in probs]

        def leave(k, j):
            kind, go = {1: (0, has_far), 3: (2, odd_or_down)}.get(k, (None, None))
            if kind is not None:

                @pl.when(go)
                def _():
                    bwd(kind, c, j, pair if kind == 2 else down).start()

        def keep(k, j, value):
            if k:
                term[k - 1, c, j] = value.astype(BF16)
                leave(k, j)
            else:
                own[c, j] = value

        order = (1, 3, 2, 0)
        for k in order:
            keep(k, 1, dot(weights[k], grad, ((1,), (0,))))
        delta = sum(
            jnp.sum(weights[k].astype(F32) * prob_grads[k], axis=0, keepdims=True) for k in sets
        )
        query_sum = None
        for k in order:
            dlogit = (probs[k] * (prob_grads[k] - delta) * scale).astype(BF16)
            keep(k, 0, dot(dlogit, query, ((1,), (0,))))
            part = dot(key_of(k), dlogit, ((0,), (0,)))
            query_sum = part if query_sum is None else query_sum + part
        result[0, c] = query_sum.T.astype(BF16)
        write(0, c).start()

    def merge(c):
        for j in (1, 0):

            @pl.when(has_both)
            def _():
                bwd(0, c, j, down).wait_recv()

            @pl.when(even_or_down)
            def _():
                bwd(2, c, j, pair).wait_recv()

            @pl.when(has_down)
            def _():
                side = jnp.where(odd, back[2, c, j].astype(F32), 0.0)
                total = term[1, c, j].astype(F32) + back[0, c, j].astype(F32) + side
                term[1, c, j] = total.astype(BF16)
                bwd(1, c, j, down).start()

    def finish(c):
        for j in (1, 0):

            @pl.when(has_up)
            def _():
                bwd(1, c, j, down).wait_recv()

            side = jnp.where(even, back[2, c, j].astype(F32), 0.0)
            result[1 + j, c] = (own[c, j] + back[1, c, j].astype(F32) + side).astype(BF16)
            write(1 + j, c).start()

    @pl.loop(0, heads + 2)
    def _(i):
        @pl.when(i + 1 < heads)
        def _():
            forward(i + 1)

        @pl.when(i < heads)
        def _():
            compute(i)

        @pl.when(jnp.logical_and(i >= 1, i <= heads))
        def _():
            merge(i - 1)

        @pl.when(i >= 2)
        def _():
            finish(i - 2)

    for index in range(lanes - 1):
        og_peer(index, lane, twin).wait_send()

    @pl.loop(0, heads)
    def _(c):
        for index in range(3):
            write(index, c).wait()
        for j in range(2):
            for present, copy in (
                (has_both, fwd(0, kv, c, j, up)),
                (has_up, fwd(1, kv, c, j, up)),
                (even_or_down, fwd(2, kv, c, j, pair)),
                (has_far, bwd(0, c, j, down)),
                (has_down, bwd(1, c, j, down)),
                (odd_or_down, bwd(2, c, j, pair)),
            ):

                @pl.when(present)
                def _():
                    copy.wait_send()


def publish_kernel(parts, *refs):
    number = (len(refs) - 2) // 2
    sources, targets = refs[:number], refs[number : 2 * number]
    held, sems = refs[2 * number :]
    rows = sources[0].shape[0] // parts
    pieces = [(a, p) for a in range(number) for p in range(parts)]

    def fetch(a, p):
        return pltpu.make_async_copy(
            sources[a].at[pl.ds(p * rows, rows)], held.at[a, p], sems.at[0, a, p]
        )

    def store(a, p):
        return pltpu.make_async_copy(
            held.at[a, p], targets[a].at[pl.ds(p * rows, rows)], sems.at[1, a, p]
        )

    for piece in pieces:
        fetch(*piece).start()
    for piece in pieces:
        fetch(*piece).wait()
        store(*piece).start()
    for piece in pieces:
        store(*piece).wait()


def publish(arrays, parts=2):
    rows, columns = arrays[0].shape
    hbm = pl.BlockSpec(memory_space=pl.ANY)
    number = len(arrays)
    return pl.pallas_call(
        functools.partial(publish_kernel, parts),
        out_shape=[jax.ShapeDtypeStruct(a.shape, a.dtype) for a in arrays],
        in_specs=[hbm] * number,
        out_specs=[hbm] * number,
        scratch_shapes=[
            pltpu.VMEM((number, parts, rows // parts, columns), arrays[0].dtype),
            pltpu.SemaphoreType.DMA((2, number, parts)),
        ],
        compiler_params=pltpu.CompilerParams(vmem_limit_bytes=60 * 2**20),
    )(*arrays)


def body(count, lanes, queries, key_rows, value_rows, out_grad, out_proj, table, active):
    rows, columns = queries.shape
    heads = columns // HDIM
    block = (heads, 2, rows, HDIM)
    vmem = pl.BlockSpec(memory_space=pltpu.VMEM)
    smem = pl.BlockSpec(memory_space=pltpu.SMEM)
    hbm = pl.BlockSpec(memory_space=pl.ANY)
    dma = pltpu.SemaphoreType.DMA
    grads = pl.pallas_call(
        functools.partial(kernel, count, lanes),
        out_shape=[jax.ShapeDtypeStruct((rows, columns), BF16)] * 3,
        in_specs=[vmem, hbm, hbm, hbm, hbm, smem, smem],
        out_specs=[hbm] * 3,
        scratch_shapes=[
            pltpu.VMEM(block, BF16),
            pltpu.VMEM((SECTIONS,) + block, BF16),
            pltpu.VMEM((SECTIONS,) + block, BF16),
            pltpu.VMEM((SECTIONS,) + block, BF16),
            pltpu.VMEM(block, F32),
            pltpu.VMEM((lanes,) + out_grad.shape, BF16),
            pltpu.VMEM(out_proj.shape, BF16),
            dma((2, heads)),
            dma((2,)),
            dma((lanes,)),
            dma((lanes,)),
            dma((SECTIONS, 2, heads)),
            dma((SECTIONS, 2, heads)),
            dma((SECTIONS, 2, heads)),
            dma((SECTIONS, 2, heads)),
            pltpu.VMEM((3, heads, rows, HDIM), BF16),
            dma((3, heads)),
        ],
        compiler_params=pltpu.CompilerParams(
            collective_id=0, has_side_effects=True, vmem_limit_bytes=60 * 2**20
        ),
    )(queries, key_rows, value_rows, out_grad, out_proj, table.T, active)
    return tuple(publish(grads))


def solution(mesh):
    return jax.shard_map(
        functools.partial(body, mesh.shape["seq"], mesh.shape["head"]),
        mesh=mesh,
        in_specs=(
            P("seq", "head"),
            P("seq", "head"),
            P("seq", "head"),
            P("seq", "head"),
            P("head", None),
            P("head", None),
            P("seq", None),
        ),
        out_specs=(P("seq", "head"), P("seq", "head"), P("seq", "head")),
        check_vma=False,
    )
```

profile of v0, /device:TPU:0, one launch (start us, length us, event | category | flops | bytes accessed | tf_op | source)
XLA Modules:
  0.0 68.5 jit_solution(12203388231294157649)
XLA Ops:
  0.6 65.7 %shard_map.94 = (bf16[256,1024]{1,0:T(8,128)(2,1)}, bf16[256,1024]{1,0:T(8,128)(2,1)}, bf16[256,1024]{1,0:T(8,128)(2,1)}) custom-call(bf16[256,1024]{1,0:T(8,128)(2,1)} %q_ref.1, bf16[256,1024]{1,0:T(8,128)(2,1)} %k_hbm.1, bf16[256,1024]{1,0:T(8,128)(2,1)} %v_hbm.1, bf16[256,512]{1,0:T(8,128)(2,1)} %og_hbm.1, bf16[1024,2048]{1,0:T(8,128)(2,1)} %proj_hbm.1, ...), custom_call_target="tpu_custom_call" | custom-call | tf_op jit(solution)/shard_map/pallas_call | solution.py:414
  66.3 2.2 %shard_map.95 = (bf16[256,1024]{1,0:T(8,128)(2,1)}, bf16[256,1024]{1,0:T(8,128)(2,1)}, bf16[256,1024]{1,0:T(8,128)(2,1)}) custom-call(bf16[256,1024]{1,0:T(8,128)(2,1)} %get-tuple-element.6.refs_0_, bf16[256,1024]{1,0:T(8,128)(2,1)} %get-tuple-element.7.refs_1_, bf16[256,1024]{1,0:T(8,128)(2,1)} %get-tuple-element.8.refs_2_), custom_call_target="tpu_custom_call" | custom-call | tf_op jit(solution)/shard_map/pallas_call | solution.py:393
where the time goes:
time: 68.8 us; the launch traced here: 68.5 us
  Pallas kernels  67.9 us (99%)
    pallas_call x1, Pallas kernels, body(): pl.pallas_call(functools.partial(kernel, count, lanes), out_shape=[jax.Sh...  65.7 us
    pallas_call x1, Pallas kernels, publish(): pl.pallas_call(functools.partial(publish_kernel, parts), out_shape=[jax.S...  2.19 us

commit v1 on v0

v1 whole, which is shorter than its diff:
```python
import functools
import math

import jax
import jax.numpy as jnp
from jax import lax
from jax.experimental import pallas as pl
from jax.experimental.pallas import tpu as pltpu
from jax.sharding import PartitionSpec as P

HDIM = 128
SECTIONS = 3
SETS = SECTIONS + 1
AHEAD = 2
FAR = 1e30
MESH = pl.DeviceIdType.MESH
BF16 = jnp.bfloat16
F32 = jnp.float32


def dot(a, b, dims):
    return lax.dot_general(a, b, (dims, ((), ())), preferred_element_type=F32)


def kernel(
    count,
    lanes,
    q_hbm,
    k_hbm,
    v_hbm,
    og_hbm,
    proj_hbm,
    table_ref,
    active_ref,
    dq_hbm,
    dk_hbm,
    dv_hbm,
    kv,
    qs,
    gs,
    og,
    proj,
    own,
    stat_out,
    stat_in,
    result,
    kv_load,
    q_load,
    load_sem,
    kv_send,
    kv_recv,
    q_send,
    q_recv,
    og_send,
    og_recv,
    lane_send,
    lane_recv,
    stat_send,
    stat_recv,
    out_sem,
):
    _, heads, _, rows, _ = kv.shape
    width = og.shape[2] // lanes
    scale = 1.0 / math.sqrt(HDIM)
    scale2 = scale / math.log(2.0)
    half, quarter, eighth = count // 2, count // 4, count // 8
    me = lax.axis_index("seq")
    lane = lax.axis_index("head")
    odd = (me // eighth) % 2 == 1
    even = jnp.logical_not(odd)
    up, down = me + quarter, me - quarter
    pair = jnp.where(odd, me - eighth, me + eighth)
    other = jnp.where(odd, me + eighth, me - eighth)
    has_up, has_down = me < count - quarter, me >= quarter
    has_far, has_near = me >= half, me < count - half
    has_both = jnp.logical_and(has_up, has_down)
    odd_or_down = jnp.logical_or(odd, has_down)
    even_or_up = jnp.logical_or(even, has_up)
    odd_and_down = jnp.logical_and(odd, has_down)
    even_and_up = jnp.logical_and(even, has_up)
    has_other = jnp.where(odd, has_up, has_down)
    twin = jnp.where(lane % 2 == 1, lane - 1, lane + 1)
    peers = [lax.rem(lane + 2 * j, lanes) for j in range(1, lanes // 2)]

    def cols(c, size):
        return pl.ds(pl.multiple_of(c * size, size), size)

    def remote(src, dst, send, recv, axis, target):
        return pltpu.make_async_remote_copy(
            src_ref=src,
            dst_ref=dst,
            send_sem=send,
            recv_sem=recv,
            device_id={axis: target},
            device_id_type=MESH,
        )

    def kv_copy(k, source, c, j, target):
        return remote(
            kv.at[j, c, source],
            kv.at[j, c, k],
            kv_send.at[k - 1, j, c],
            kv_recv.at[k - 1, j, c],
            "seq",
            target,
        )

    def q_copy(k, source, c, target):
        return remote(
            qs.at[c, source],
            qs.at[c, k],
            q_send.at[k - 1, c],
            q_recv.at[k - 1, c],
            "seq",
            target,
        )

    def og_copy(k, source, target):
        return remote(
            og.at[source, :, cols(lane, width)],
            og.at[k, :, cols(lane, width)],
            og_send.at[k - 1],
            og_recv.at[k - 1],
            "seq",
            target,
        )

    def lane_copy(k, index, shard, target):
        return remote(
            og.at[k, :, cols(shard, width)],
            og.at[k, :, cols(shard, width)],
            lane_send.at[k, index],
            lane_recv.at[k, shard],
            "head",
            target,
        )

    def stat_copy(k, c, target):
        return remote(
            stat_out.at[c, k - 1],
            stat_in.at[c, k - 1],
            stat_send.at[k - 1, c],
            stat_recv.at[k - 1, c],
            "seq",
            target,
        )

    def load_kv(c, j):
        return pltpu.make_async_copy(
            (k_hbm, v_hbm)[j].at[:, cols(c, HDIM)], kv.at[j, c, 0], kv_load.at[j, c]
        )

    def load_q(c):
        return pltpu.make_async_copy(q_hbm.at[:, cols(c, HDIM)], qs.at[c, 0], q_load.at[c])

    def write(index, c):
        target = (dq_hbm, dk_hbm, dv_hbm)[index]
        return pltpu.make_async_copy(
            result.at[index, c], target.at[:, cols(c, HDIM)], out_sem.at[index, c]
        )

    load_og = pltpu.make_async_copy(og_hbm, og.at[0, :, cols(lane, width)], load_sem.at[0])
    load_proj = pltpu.make_async_copy(proj_hbm, proj, load_sem.at[1])
    load_og.start()

    @pl.loop(0, heads)
    def _(c):
        for j in range(2):
            load_kv(c, j).start()
        load_q(c).start()

    load_proj.start()

    barrier = pltpu.get_barrier_semaphore()
    arrivals = jnp.int32(2 + len(peers))
    for peer in [twin] + peers:
        pl.semaphore_signal(barrier, inc=1, device_id={"head": peer}, device_id_type=MESH)
    pl.semaphore_signal(barrier, inc=1, device_id={"seq": pair}, device_id_type=MESH)
    for present, target in (
        (has_up, up),
        (has_down, down),
        (has_far, me - half),
        (has_near, me + half),
        (has_other, other),
    ):
        arrivals = arrivals + present.astype(jnp.int32)

        @pl.when(present)
        def _():
            pl.semaphore_signal(barrier, inc=1, device_id={"seq": target}, device_id_type=MESH)

    pl.semaphore_wait(barrier, arrivals)

    def gather_start(k):
        for j, peer in enumerate(peers):
            lane_copy(k, 1 + j, lane, peer).start()
        lane_copy(k, 0, lane, twin).start()

    def gather_pass(k):
        for j, peer in enumerate(peers):
            lane_copy(k, 1 + j, peer, lane).wait_recv()
            lane_copy(k, len(peers) + 1 + j, peer, twin).start()

    def gather_end(k):
        lane_copy(k, 0, twin, lane).wait_recv()
        for j in range(len(peers)):
            shard = lax.rem(twin + 2 * (j + 1), lanes)
            lane_copy(k, len(peers) + 1 + j, shard, lane).wait_recv()

    def send_kv(c):
        for j in range(2):
            load_kv(c, j).wait()

            @pl.when(has_up)
            def _():
                kv_copy(2, 0, c, j, up).start()

            @pl.when(even)
            def _():
                kv_copy(3, 0, c, j, pair).start()

    def send_q(c):
        load_q(c).wait()

        @pl.when(has_down)
        def _():
            q_copy(2, 0, c, down).start()

        @pl.when(odd)
        def _():
            q_copy(3, 0, c, pair).start()

    def relay_kv(c):
        for j in range(2):

            @pl.when(has_down)
            def _():
                kv_copy(2, 0, c, j, up).wait_recv()

            @pl.when(has_both)
            def _():
                kv_copy(1, 2, c, j, up).start()

            @pl.when(odd_and_down)
            def _():
                kv_copy(3, 2, c, j, pair).start()

        @pl.when(c + AHEAD < heads)
        def _():
            send_kv(c + AHEAD)

    def relay_q(c):
        @pl.when(has_up)
        def _():
            q_copy(2, 0, c, down).wait_recv()

        @pl.when(has_both)
        def _():
            q_copy(1, 2, c, down).start()

        @pl.when(even_and_up)
        def _():
            q_copy(3, 2, c, pair).start()

    load_og.wait()
    gather_start(0)

    @pl.when(has_down)
    def _():
        og_copy(2, 0, down).start()

    @pl.when(odd)
    def _():
        og_copy(3, 0, pair).start()

    for c in range(AHEAD):
        send_kv(jnp.int32(c))
    here = {1: has_near, 2: has_up, 3: even_or_up}
    reach = {1: has_far, 2: has_down, 3: odd_or_down}
    for k in range(1, SETS):

        @pl.when(jnp.logical_not(reach[k]))
        def _():
            @pl.loop(0, heads)
            def _(c):
                for j in range(2):
                    kv[j, c, k] = jnp.zeros((rows, HDIM), BF16)

        @pl.when(jnp.logical_not(here[k]))
        def _():
            @pl.loop(0, heads)
            def _(c):
                qs[c, k] = jnp.zeros((rows, HDIM), BF16)
                gs[c, k] = jnp.zeros((rows, HDIM), BF16)
                stat_in[c, k - 1] = jnp.full((2, rows), FAR, F32)

    relay_kv(jnp.int32(0))

    def project(k):
        @pl.loop(0, heads // 2)
        def _(t):
            tile = proj[cols(t, 2 * HDIM), :]
            grad = dot(og[k], tile, ((1,), (1,))).astype(BF16)
            gs[2 * t, k] = grad[:, :HDIM]
            gs[2 * t + 1, k] = grad[:, HDIM:]

    gather_pass(0)
    load_proj.wait()
    gather_end(0)
    project(0)

    key_index = lax.broadcasted_iota(jnp.int32, (rows, rows), 0)
    query_index = lax.broadcasted_iota(jnp.int32, (rows, rows), 1)

    def attend(c):
        query, grad = qs[c, 0], gs[c, 0]
        raw = dot(kv[0, c].reshape(SETS * rows, HDIM), query, ((1,), (1,))) * scale2
        prob_grad = dot(kv[1, c].reshape(SETS * rows, HDIM), grad, ((1,), (1,)))
        logits = [raw[k * rows : (k + 1) * rows] for k in range(SETS)]
        prob_grads = [prob_grad[k * rows : (k + 1) * rows] for k in range(SETS)]
        logits[0] = jnp.where(key_index <= query_index, logits[0], -FAR)
        top = jnp.max(logits[0], axis=0, keepdims=True)
        usable = {}
        for k in range(1, SETS):
            usable[k] = jnp.logical_and(
                table_ref[k - 1, c] * active_ref[0, k - 1] > 0, me >= count // 2**k
            )
            best = jnp.max(logits[k], axis=0, keepdims=True)
            top = jnp.maximum(top, best + jnp.where(usable[k], 0.0, -FAR).astype(F32))
        total, weighted, exps = 0.0, 0.0, []
        for k in range(SETS):
            shift = top if k == 0 else top + jnp.where(usable[k], 0.0, FAR).astype(F32)
            exps.append(jnp.exp2(logits[k] - shift))
            total = total + jnp.sum(exps[k], axis=0, keepdims=True)
            weighted = weighted + jnp.sum(exps[k] * prob_grads[k], axis=0, keepdims=True)
        inverse = 1.0 / total
        delta = weighted * inverse
        norm = top + jnp.log2(total)
        for k in range(1, SETS):
            hidden = jnp.where(active_ref[0, k - 1] > 0, 0.0, FAR).astype(F32)
            stat_out[c, k - 1] = jnp.concatenate([norm + hidden, delta], axis=0)

        probs = exps[0] * inverse
        dlogit = (probs * (prob_grads[0] - delta)).astype(BF16)
        own[0, c] = dot(dlogit, query, ((1,), (0,))) * scale
        own[1, c] = dot(probs.astype(BF16), grad, ((1,), (0,)))
        others = jnp.concatenate(
            [(exps[k] * (prob_grads[k] - delta)).astype(BF16) for k in range(1, SETS)], axis=0
        )
        keys = kv[0, c, 1:].reshape(SECTIONS * rows, HDIM)
        far = dot(keys, others, ((0,), (0,))) * inverse
        near = dot(kv[0, c, 0], dlogit, ((0,), (0,)))
        result[0, c] = ((far + near) * scale).T.astype(BF16)

    def tell(c):
        for k, go, span in ((1, has_far, half), (2, has_down, quarter), (3, odd_or_down, eighth)):

            @pl.when(go)
            def _():
                stat_copy(k, c, me - span).start()

        write(0, c).start()

    def collect(c):
        queries = qs[c, 1:].reshape(SECTIONS * rows, HDIM)
        grads = gs[c, 1:].reshape(SECTIONS * rows, HDIM)
        raw = dot(kv[0, c, 0], queries, ((1,), (1,))) * scale2
        prob_grad = dot(kv[1, c, 0], grads, ((1,), (1,)))
        weights, dlogits = [], []
        for k in range(1, SETS):
            part = slice((k - 1) * rows, k * rows)
            hidden = jnp.where(table_ref[k - 1, c] > 0, 0.0, FAR).astype(F32)
            probs = jnp.exp2(raw[:, part] - (stat_in[c, k - 1, 0:1] + hidden))
            weights.append(probs.astype(BF16))
            dlogits.append((probs * (prob_grad[:, part] - stat_in[c, k - 1, 1:2])).astype(BF16))
        key = dot(jnp.concatenate(dlogits, axis=1), queries, ((1,), (0,)))
        value = dot(jnp.concatenate(weights, axis=1), grads, ((1,), (0,)))
        result[1, c] = (own[0, c] + key * scale).astype(BF16)
        result[2, c] = (own[1, c] + value).astype(BF16)

    def finish(c):
        for k, source in ((1, half), (2, quarter), (3, eighth)):

            @pl.when(here[k])
            def _():
                stat_copy(k, c, me + source).wait_recv()

        for k in (1, 3):

            @pl.when(here[k])
            def _():
                q_copy(k, 0, c, me).wait_recv()

        collect(c)
        for index in (1, 2):
            write(index, c).start()

    def arrive(k):
        @pl.when(here[k])
        def _():
            og_copy(k, 0, me).wait_recv()
            if k == 2:

                @pl.when(has_both)
                def _():
                    og_copy(1, 2, down).start()

                @pl.when(even)
                def _():
                    og_copy(3, 2, pair).start()

            gather_start(k)

    def hand_on(k):
        @pl.when(here[k])
        def _():
            gather_pass(k)

    def take(k):
        @pl.when(here[k])
        def _():
            gather_end(k)
            project(k)

    middle = heads // 2

    @pl.loop(0, heads)
    def _(i):
        @pl.when(i < middle)
        def _():
            send_q(2 * i)
            send_q(2 * i + 1)

        for step, action, k in (
            (0, arrive, 2),
            (1, hand_on, 2),
            (1, arrive, 3),
            (2, hand_on, 3),
            (2, arrive, 1),
            (3, hand_on, 1),
        ):

            @pl.when(i == step)
            def _():
                action(k)

        @pl.when(i + 1 < heads)
        def _():
            relay_kv(i + 1)

        @pl.when(jnp.logical_and(i >= 2, i < 2 + middle))
        def _():
            relay_q(2 * (i - 2))
            relay_q(2 * (i - 2) + 1)

        for j in range(2):
            for k in (1, 3):

                @pl.when(reach[k])
                def _():
                    kv_copy(k, 0, i, j, me).wait_recv()

        attend(i)
        tell(i)
        for step, k in ((2, 2), (3, 3), (4, 1)):

            @pl.when(i == step)
            def _():
                take(k)

        first = 2 * (i - middle)

        @pl.when(i >= middle)
        def _():
            @pl.loop(first, jnp.minimum(first + 2, heads - 1))
            def _(c):
                finish(c)

    finish(jnp.int32(heads - 1))

    def drain(k):
        for index in range(lanes - 1):
            lane_copy(k, index, lane, twin).wait_send()

    drain(0)
    for k in range(1, SETS):

        @pl.when(here[k])
        def _():
            drain(k)

    sent = {1: has_both, 2: has_down, 3: jnp.logical_or(odd, has_up)}
    for k in range(1, SETS):

        @pl.when(sent[k])
        def _():
            og_copy(k, 0, pair).wait_send()

    @pl.loop(0, heads)
    def _(c):
        for index in range(3):
            write(index, c).wait()
        for present, copy in (
            (has_both, q_copy(1, 2, c, down)),
            (has_down, q_copy(2, 0, c, down)),
            (jnp.logical_or(odd, has_up), q_copy(3, 0, c, pair)),
            (has_far, stat_copy(1, c, pair)),
            (has_down, stat_copy(2, c, pair)),
            (odd_or_down, stat_copy(3, c, pair)),
        ):

            @pl.when(present)
            def _():
                copy.wait_send()

        for j in range(2):
            for present, k in ((has_both, 1), (has_up, 2), (jnp.logical_or(even, has_down), 3)):

                @pl.when(present)
                def _():
                    kv_copy(k, 0, c, j, up).wait_send()


def publish_kernel(parts, *refs):
    number = (len(refs) - 2) // 2
    sources, targets = refs[:number], refs[number : 2 * number]
    held, sems = refs[2 * number :]
    rows = sources[0].shape[0] // parts
    pieces = [(a, p) for a in range(number) for p in range(parts)]

    def fetch(a, p):
        return pltpu.make_async_copy(
            sources[a].at[pl.ds(p * rows, rows)], held.at[a, p], sems.at[0, a, p]
        )

    def store(a, p):
        return pltpu.make_async_copy(
            held.at[a, p], targets[a].at[pl.ds(p * rows, rows)], sems.at[1, a, p]
        )

    for piece in pieces:
        fetch(*piece).start()
    for piece in pieces:
        fetch(*piece).wait()
        store(*piece).start()
    for piece in pieces:
        store(*piece).wait()


def publish(arrays, parts=2):
    rows, columns = arrays[0].shape
    hbm = pl.BlockSpec(memory_space=pl.ANY)
    number = len(arrays)
    return pl.pallas_call(
        functools.partial(publish_kernel, parts),
        out_shape=[jax.ShapeDtypeStruct(a.shape, a.dtype) for a in arrays],
        in_specs=[hbm] * number,
        out_specs=[hbm] * number,
        scratch_shapes=[
            pltpu.VMEM((number, parts, rows // parts, columns), arrays[0].dtype),
            pltpu.SemaphoreType.DMA((2, number, parts)),
        ],
        compiler_params=pltpu.CompilerParams(vmem_limit_bytes=60 * 2**20),
    )(*arrays)


def body(count, lanes, queries, key_rows, value_rows, out_grad, out_proj, table, active):
    rows, columns = queries.shape
    heads = columns // HDIM
    smem = pl.BlockSpec(memory_space=pltpu.SMEM)
    hbm = pl.BlockSpec(memory_space=pl.ANY)
    dma = pltpu.SemaphoreType.DMA
    grads = pl.pallas_call(
        functools.partial(kernel, count, lanes),
        out_shape=[jax.ShapeDtypeStruct((rows, columns), BF16)] * 3,
        in_specs=[hbm] * 5 + [smem] * 2,
        out_specs=[hbm] * 3,
        scratch_shapes=[
            pltpu.VMEM((2, heads, SETS, rows, HDIM), BF16),
            pltpu.VMEM((heads, SETS, rows, HDIM), BF16),
            pltpu.VMEM((heads, SETS, rows, HDIM), BF16),
            pltpu.VMEM((SETS, rows, out_proj.shape[1]), BF16),
            pltpu.VMEM(out_proj.shape, BF16),
            pltpu.VMEM((2, heads, rows, HDIM), F32),
            pltpu.VMEM((heads, SECTIONS, 2, rows), F32),
            pltpu.VMEM((heads, SECTIONS, 2, rows), F32),
            pltpu.VMEM((3, heads, rows, HDIM), BF16),
            dma((2, heads)),
            dma((heads,)),
            dma((2,)),
            dma((SECTIONS, 2, heads)),
            dma((SECTIONS, 2, heads)),
            dma((SECTIONS, heads)),
            dma((SECTIONS, heads)),
            dma((SECTIONS,)),
            dma((SECTIONS,)),
            dma((SETS, lanes)),
            dma((SETS, lanes)),
            dma((SECTIONS, heads)),
            dma((SECTIONS, heads)),
            dma((3, heads)),
        ],
        compiler_params=pltpu.CompilerParams(
            collective_id=0, has_side_effects=True, vmem_limit_bytes=60 * 2**20
        ),
    )(queries, key_rows, value_rows, out_grad, out_proj, table.T, active)
    return tuple(publish(grads))


def solution(mesh):
    return jax.shard_map(
        functools.partial(body, mesh.shape["seq"], mesh.shape["head"]),
        mesh=mesh,
        in_specs=(
            P("seq", "head"),
            P("seq", "head"),
            P("seq", "head"),
            P("seq", "head"),
            P("head", None),
            P("head", None),
            P("seq", None),
        ),
        out_specs=(P("seq", "head"), P("seq", "head"), P("seq", "head")),
        check_vma=False,
    )
```

time: 68.8 us -> 67.8 us (0.985)
  Pallas kernels: 67.9 us -> 67 us
    pallas_call x1, Pallas kernels: 65.7 us -> 64.8 us  [body(): pl.pallas_call(functools.partial(kernel, count, lanes), out_shape=[jax.Sh...]
where the time goes in v1:
time: 67.8 us; the launch traced here: 67.6 us
  Pallas kernels  67 us (99%)
    pallas_call x1, Pallas kernels, body(): pl.pallas_call(functools.partial(kernel, count, lanes), out_shape=[jax.Sh...  64.8 us
    pallas_call x1, Pallas kernels, publish(): pl.pallas_call(functools.partial(publish_kernel, parts), out_shape=[jax.S...  2.19 us

profile of v1, /device:TPU:0, one launch (start us, length us, event | category | flops | bytes accessed | tf_op | source)
XLA Modules:
  0.0 67.6 jit_solution(4111231335364777369)
XLA Ops:
  0.6 64.8 %shard_map.94 = (bf16[256,1024]{1,0:T(8,128)(2,1)}, bf16[256,1024]{1,0:T(8,128)(2,1)}, bf16[256,1024]{1,0:T(8,128)(2,1)}) custom-call(bf16[256,1024]{1,0:T(8,128)(2,1)} %q_hbm.1, bf16[256,1024]{1,0:T(8,128)(2,1)} %k_hbm.1, bf16[256,1024]{1,0:T(8,128)(2,1)} %v_hbm.1, bf16[256,512]{1,0:T(8,128)(2,1)} %og_hbm.1, bf16[1024,2048]{1,0:T(8,128)(2,1)} %proj_hbm.1, ...), custom_call_target="tpu_custom_call" | custom-call | tf_op jit(solution)/shard_map/pallas_call | solution.py:573
  65.4 2.2 %shard_map.95 = (bf16[256,1024]{1,0:T(8,128)(2,1)}, bf16[256,1024]{1,0:T(8,128)(2,1)}, bf16[256,1024]{1,0:T(8,128)(2,1)}) custom-call(bf16[256,1024]{1,0:T(8,128)(2,1)} %get-tuple-element.6.refs_0_, bf16[256,1024]{1,0:T(8,128)(2,1)} %get-tuple-element.7.refs_1_, bf16[256,1024]{1,0:T(8,128)(2,1)} %get-tuple-element.8.refs_2_), custom_call_target="tpu_custom_call" | custom-call | tf_op jit(solution)/shard_map/pallas_call | solution.py:554

commit v2 on v1

v2 whole, which is shorter than its diff:
```python
import functools
import math

import jax
import jax.numpy as jnp
from jax import lax
from jax.experimental import pallas as pl
from jax.experimental.pallas import tpu as pltpu
from jax.sharding import PartitionSpec as P

HDIM = 128
SECTIONS = 3
SETS = SECTIONS + 1
ASKED = 2
EARLY = 2
FAR = 1e30
MESH = pl.DeviceIdType.MESH
BF16 = jnp.bfloat16
F32 = jnp.float32


def dot(a, b, dims):
    return lax.dot_general(a, b, (dims, ((), ())), preferred_element_type=F32)


def kernel(
    count,
    lanes,
    q_hbm,
    k_hbm,
    v_hbm,
    og_hbm,
    proj_hbm,
    table_ref,
    active_ref,
    dq_ref,
    dk_ref,
    dv_ref,
    kv,
    qs,
    gs,
    og,
    proj,
    own,
    stat_out,
    stat_in,
    part_own,
    part_out,
    part_in,
    stat_own,
    held,
    term,
    back,
    kv_load,
    q_load,
    load_sem,
    kv_send,
    kv_recv,
    q_send,
    q_recv,
    og_send,
    og_recv,
    lane_send,
    lane_recv,
    stat_send,
    stat_recv,
    part_send,
    part_recv,
    term_send,
    term_recv,
):
    _, heads, _, rows, _ = kv.shape
    width = og.shape[2] // lanes
    piece = rows // 2
    keyed = heads - ASKED
    scale = 1.0 / math.sqrt(HDIM)
    scale2 = scale / math.log(2.0)
    half, quarter, eighth = count // 2, count // 4, count // 8
    me = lax.axis_index("seq")
    lane = lax.axis_index("head")
    odd = (me // eighth) % 2 == 1
    even = jnp.logical_not(odd)
    up, down = me + quarter, me - quarter
    pair = jnp.where(odd, me - eighth, me + eighth)
    other = jnp.where(odd, me + eighth, me - eighth)
    has_up, has_down = me < count - quarter, me >= quarter
    has_far, has_near = me >= half, me < count - half
    has_both = jnp.logical_and(has_up, has_down)
    odd_or_down = jnp.logical_or(odd, has_down)
    even_or_up = jnp.logical_or(even, has_up)
    odd_and_down = jnp.logical_and(odd, has_down)
    even_and_up = jnp.logical_and(even, has_up)
    has_other = jnp.where(odd, has_up, has_down)
    twin = jnp.where(lane % 2 == 1, lane - 1, lane + 1)
    peers = [lax.rem(lane + 2 * j, lanes) for j in range(1, lanes // 2)]

    def cols(c, size):
        return pl.ds(pl.multiple_of(c * size, size), size)

    def remote(src, dst, send, recv, axis, target):
        return pltpu.make_async_remote_copy(
            src_ref=src,
            dst_ref=dst,
            send_sem=send,
            recv_sem=recv,
            device_id={axis: target},
            device_id_type=MESH,
        )

    def kv_copy(k, source, c, target):
        return remote(
            kv.at[:, c, source],
            kv.at[:, c, k],
            kv_send.at[k - 1],
            kv_recv.at[k - 1, c],
            "seq",
            target,
        )

    def q_copy(k, source, c, target):
        return remote(
            qs.at[c, source],
            qs.at[c, k],
            q_send.at[k - 1],
            q_recv.at[k - 1, c],
            "seq",
            target,
        )

    def og_copy(k, source, p, target):
        part = pl.ds(p * piece, piece)
        return remote(
            og.at[source, part, cols(lane, width)],
            og.at[k, part, cols(lane, width)],
            og_send.at[k - 1],
            og_recv.at[k - 1, p],
            "seq",
            target,
        )

    def lane_copy(k, shard, p, target):
        part = og.at[k, pl.ds(p * piece, piece), cols(shard, width)]
        return remote(
            part, part, lane_send.at[k], lane_recv.at[k, p, shard], "head", target
        )

    def part_copy(k, c, target):
        return remote(
            part_out.at[c - keyed, k - 1],
            part_in.at[c - keyed, k - 1],
            part_send.at[k - 1],
            part_recv.at[k - 1, c - keyed],
            "seq",
            target,
        )

    def term_copy(k, c, target):
        return remote(
            term.at[c - keyed, k - 1],
            back.at[c - keyed, k - 1],
            term_send.at[k - 1],
            term_recv.at[k - 1, c - keyed],
            "seq",
            target,
        )

    def stat_copy(k, c, target):
        return remote(
            stat_out.at[c, k - 1],
            stat_in.at[c, k - 1],
            stat_send.at[k - 1],
            stat_recv.at[k - 1, c],
            "seq",
            target,
        )

    def load_kv(c, j):
        return pltpu.make_async_copy(
            (k_hbm, v_hbm)[j].at[:, cols(c, HDIM)], kv.at[j, c, 0], kv_load.at[j, c]
        )

    def load_q(c):
        return pltpu.make_async_copy(q_hbm.at[:, cols(c, HDIM)], qs.at[c, 0], q_load.at[c])

    barrier = pltpu.get_barrier_semaphore()
    arrivals = jnp.int32(2 + len(peers))
    for peer in [twin] + peers:
        pl.semaphore_signal(barrier, inc=1, device_id={"head": peer}, device_id_type=MESH)
    pl.semaphore_signal(barrier, inc=1, device_id={"seq": pair}, device_id_type=MESH)
    for present, target in (
        (has_up, up),
        (has_down, down),
        (has_far, me - half),
        (has_near, me + half),
        (has_other, other),
    ):
        arrivals = arrivals + present.astype(jnp.int32)

        @pl.when(present)
        def _():
            pl.semaphore_signal(barrier, inc=1, device_id={"seq": target}, device_id_type=MESH)

    load_og = pltpu.make_async_copy(og_hbm, og.at[0, :, cols(lane, width)], load_sem.at[0])

    def load_proj(t):
        part = pl.ds(t * 2 * HDIM, 2 * HDIM)
        return pltpu.make_async_copy(proj_hbm.at[part], proj.at[part], load_sem.at[1 + t])

    load_og.start()
    for c in range(EARLY):
        for j in range(2):
            load_kv(c, j).start()

    pl.semaphore_wait(barrier, arrivals)

    def gather_start(k, p):
        for peer in peers:
            lane_copy(k, lane, p, peer).start()
        lane_copy(k, lane, p, twin).start()

    def gather_pass(k):
        for p in range(2):
            for peer in peers:
                lane_copy(k, peer, p, lane).wait_recv()
                lane_copy(k, peer, p, twin).start()

    def gather_end(k):
        for p in range(2):
            lane_copy(k, twin, p, lane).wait_recv()
            for j in range(len(peers)):
                shard = lax.rem(twin + 2 * (j + 1), lanes)
                lane_copy(k, shard, p, lane).wait_recv()

    loaded = set()

    def ready(c):
        if c not in loaded:
            loaded.add(c)
            for copy in [load_q(c)] if c < heads else map(load_proj, range(heads // 2)):
                copy.wait()

    def send_kv(c):
        for j in range(2):
            load_kv(c, j).wait()

        @pl.when(has_up)
        def _():
            kv_copy(2, 0, c, up).start()

        @pl.when(even)
        def _():
            kv_copy(3, 0, c, pair).start()

    def send_q(c):
        ready(c)

        @pl.when(has_down)
        def _():
            q_copy(2, 0, c, down).start()

    def side_q(c):
        ready(c)

        @pl.when(odd)
        def _():
            q_copy(3, 0, c, pair).start()

    def relay_kv(c):
        @pl.when(has_down)
        def _():
            kv_copy(2, 0, c, up).wait_recv()

        @pl.when(has_both)
        def _():
            kv_copy(1, 2, c, up).start()

        @pl.when(odd_and_down)
        def _():
            kv_copy(3, 2, c, pair).start()

    def relay_q(c):
        @pl.when(has_up)
        def _():
            q_copy(2, 0, c, down).wait_recv()

        @pl.when(has_both)
        def _():
            q_copy(1, 2, c, down).start()

        @pl.when(even_and_up)
        def _():
            q_copy(3, 2, c, pair).start()

    load_og.wait()
    for p in range(2):
        gather_start(0, p)

        @pl.when(has_down)
        def _():
            og_copy(2, 0, p, down).start()

        @pl.when(odd)
        def _():
            og_copy(3, 0, p, pair).start()

    for c in range(EARLY, heads):
        for j in range(2):
            load_kv(c, j).start()

    for c in range(heads):
        load_q(c).start()

    here = {0: me >= 0, 1: has_near, 2: has_up, 3: even_or_up}
    reach = {1: has_far, 2: has_down, 3: odd_or_down}
    for k in range(1, SETS):

        @pl.when(jnp.logical_not(reach[k]))
        def _():
            @pl.loop(0, keyed)
            def _(c):
                for j in range(2):
                    kv[j, c, k] = jnp.zeros((rows, HDIM), BF16)

            for c in range(ASKED):
                part_in[c, k - 1] = jnp.full((3, rows), -FAR, F32)

        @pl.when(jnp.logical_not(here[k]))
        def _():
            @pl.loop(0, heads)
            def _(c):
                qs[c, k] = jnp.zeros((rows, HDIM), BF16)
                gs[c, k] = jnp.zeros((rows, HDIM), BF16)
                stat_in[c, k - 1] = jnp.full((2, rows), FAR, F32)

    for k, present in ((1, has_both), (2, has_down), (3, jnp.logical_or(odd, has_up))):

        @pl.when(jnp.logical_not(present))
        def _():
            for c in range(ASKED):
                back[c, k - 1] = jnp.zeros((HDIM, rows), BF16)

    def project(k, low, high):
        @pl.loop(low // 2, high // 2)
        def _(t):
            tile = proj[cols(t, 2 * HDIM), :]
            grad = dot(og[k], tile, ((1,), (1,))).astype(BF16)
            gs[2 * t, k] = grad[:, :HDIM]
            gs[2 * t + 1, k] = grad[:, HDIM:]

    key_index = lax.broadcasted_iota(jnp.int32, (rows, rows), 0)
    query_index = lax.broadcasted_iota(jnp.int32, (rows, rows), 1)

    def attend(c):
        ready(c)
        for k in (1, 3):

            @pl.when(reach[k])
            def _():
                kv_copy(k, 0, c, me).wait_recv()

        query, grad = qs[c, 0], gs[c, 0]
        raw = dot(kv[0, c].reshape(SETS * rows, HDIM), query, ((1,), (1,))) * scale2
        prob_grad = dot(kv[1, c].reshape(SETS * rows, HDIM), grad, ((1,), (1,)))
        logits = [raw[k * rows : (k + 1) * rows] for k in range(SETS)]
        prob_grads = [prob_grad[k * rows : (k + 1) * rows] for k in range(SETS)]
        logits[0] = jnp.where(key_index <= query_index, logits[0], -FAR)
        top = jnp.max(logits[0], axis=0, keepdims=True)
        usable = {}
        for k in range(1, SETS):
            usable[k] = jnp.logical_and(
                table_ref[k - 1, c] * active_ref[0, k - 1] > 0, me >= count // 2**k
            )
            best = jnp.max(logits[k], axis=0, keepdims=True)
            top = jnp.maximum(top, best + jnp.where(usable[k], 0.0, -FAR).astype(F32))
        total, weighted, exps = 0.0, 0.0, []
        for k in range(SETS):
            shift = top if k == 0 else top + jnp.where(usable[k], 0.0, FAR).astype(F32)
            exps.append(jnp.exp2(logits[k] - shift))
            total = total + jnp.sum(exps[k], axis=0, keepdims=True)
            weighted = weighted + jnp.sum(exps[k] * prob_grads[k], axis=0, keepdims=True)
        inverse = 1.0 / total
        delta = weighted * inverse
        norm = top + jnp.log2(total)
        for k in range(1, SETS):
            hidden = jnp.where(active_ref[0, k - 1] > 0, 0.0, FAR).astype(F32)
            stat_out[c, k - 1] = jnp.concatenate([norm + hidden, delta], axis=0)

        probs = exps[0] * inverse
        dlogit = (probs * (prob_grads[0] - delta)).astype(BF16)
        own[0, c] = dot(dlogit, query, ((1,), (0,))) * scale
        own[1, c] = dot(probs.astype(BF16), grad, ((1,), (0,)))
        others = jnp.concatenate(
            [(exps[k] * (prob_grads[k] - delta)).astype(BF16) for k in range(1, SETS)], axis=0
        )
        keys = kv[0, c, 1:].reshape(SECTIONS * rows, HDIM)
        far = dot(keys, others, ((0,), (0,))) * inverse
        near = dot(kv[0, c, 0], dlogit, ((0,), (0,)))
        dq_ref[:, cols(c, HDIM)] = ((far + near) * scale).T.astype(BF16)
        tell(c)

    def tell(c):
        for k, go, span in ((1, has_far, half), (2, has_down, quarter), (3, odd_or_down, eighth)):

            @pl.when(go)
            def _():
                stat_copy(k, c, me - span).start()

    def collect(c):
        queries = qs[c, 1:].reshape(SECTIONS * rows, HDIM)
        grads = gs[c, 1:].reshape(SECTIONS * rows, HDIM)
        raw = dot(kv[0, c, 0], queries, ((1,), (1,))) * scale2
        prob_grad = dot(kv[1, c, 0], grads, ((1,), (1,)))
        weights, dlogits = [], []
        for k in range(1, SETS):
            part = slice((k - 1) * rows, k * rows)
            hidden = jnp.where(table_ref[k - 1, c] > 0, 0.0, FAR).astype(F32)
            probs = jnp.exp2(raw[:, part] - (stat_in[c, k - 1, 0:1] + hidden))
            weights.append(probs.astype(BF16))
            dlogits.append((probs * (prob_grad[:, part] - stat_in[c, k - 1, 1:2])).astype(BF16))
        key = dot(jnp.concatenate(dlogits, axis=1), queries, ((1,), (0,)))
        value = dot(jnp.concatenate(weights, axis=1), grads, ((1,), (0,)))
        dk_ref[:, cols(c, HDIM)] = (own[0, c] + key * scale).astype(BF16)
        dv_ref[:, cols(c, HDIM)] = (own[1, c] + value).astype(BF16)

    def finish(c):
        for k, source in ((1, half), (2, quarter), (3, eighth)):

            @pl.when(here[k])
            def _():
                stat_copy(k, c, me + source).wait_recv()

        for k in (1, 3):

            @pl.when(here[k])
            def _():
                q_copy(k, 0, c, me).wait_recv()

        collect(c)

    def arrive(k, p):
        @pl.when(here[k])
        def _():
            og_copy(k, 0, p, me).wait_recv()
            if k == 2:

                @pl.when(has_both)
                def _():
                    og_copy(1, 2, p, down).start()

                @pl.when(even)
                def _():
                    og_copy(3, 2, p, pair).start()

            gather_start(k, p)

    def hand_on(k):
        @pl.when(here[k])
        def _():
            gather_pass(k)

    def take(k, low=0, high=heads):
        ready(heads)

        @pl.when(here[k])
        def _():
            gather_end(k)
            project(k, low, high)

    def some(k):
        take(k, keyed, heads)

    def rest(k):
        @pl.when(here[k])
        def _():
            project(k, 0, keyed)

    def ask(c):
        for k in (1, 3):

            @pl.when(here[k])
            def _():
                q_copy(k, 0, c, me).wait_recv()

        for j in range(2):
            load_kv(c, j).wait()
        raw = dot(kv[0, c, 0], qs[c].reshape(SETS * rows, HDIM), ((1,), (1,))) * scale2
        prob_grad = dot(kv[1, c, 0], gs[c].reshape(SETS * rows, HDIM), ((1,), (1,)))
        for k in range(SETS):
            part = slice(k * rows, (k + 1) * rows)
            logits = raw[:, part]
            if k == 0:
                logits = jnp.where(key_index <= query_index, logits, -FAR)
            top = jnp.max(logits, axis=0, keepdims=True)
            exps = jnp.exp2(logits - top)
            total = jnp.sum(exps, axis=0, keepdims=True)
            weighted = jnp.sum(exps * prob_grad[:, part], axis=0, keepdims=True)
            if k == 0:
                part_own[c - keyed] = jnp.concatenate([top, total, weighted], axis=0)
            else:
                top = top + jnp.where(table_ref[k - 1, c] > 0, 0.0, -FAR).astype(F32)
                part_out[c - keyed, k - 1] = jnp.concatenate([top, total, weighted], axis=0)
        for k, span in ((1, half), (2, quarter), (3, eighth)):

            @pl.when(here[k])
            def _():
                part_copy(k, c, me + span).start()

    def combine(c):
        for k in range(1, SETS):

            @pl.when(reach[k])
            def _():
                part_copy(k, c, me).wait_recv()

        h = c - keyed
        tops, parts = [part_own[h, 0:1]], [(part_own[h, 1:2], part_own[h, 2:3])]
        for k in range(1, SETS):
            usable = jnp.logical_and(active_ref[0, k - 1] > 0, me >= count // 2**k)
            hidden = jnp.where(usable, 0.0, -FAR).astype(F32)
            tops.append(part_in[h, k - 1, 0:1] + hidden)
            sums = part_in[h, k - 1]
            parts.append((jnp.where(usable, sums[1:2], 0.0), jnp.where(usable, sums[2:3], 0.0)))
        top = functools.reduce(jnp.maximum, tops)
        shares = [jnp.exp2(x - top) for x in tops]
        total = sum(share * part[0] for share, part in zip(shares, parts))
        delta = sum(share * part[1] for share, part in zip(shares, parts)) / total
        norm = top + jnp.log2(total)
        stat_own[h] = jnp.concatenate([norm, delta], axis=0)
        for k in range(1, SETS):
            hidden = jnp.where(active_ref[0, k - 1] > 0, 0.0, FAR).astype(F32)
            stat_out[c, k - 1] = jnp.concatenate([norm + hidden, delta], axis=0)
        tell(c)

    def answer(c):
        for k, span in ((1, half), (2, quarter), (3, eighth)):

            @pl.when(here[k])
            def _():
                stat_copy(k, c, me + span).wait_recv()

        h = c - keyed
        queries = qs[c].reshape(SETS * rows, HDIM)
        grads = gs[c].reshape(SETS * rows, HDIM)
        raw = dot(kv[0, c, 0], queries, ((1,), (1,))) * scale2
        prob_grad = dot(kv[1, c, 0], grads, ((1,), (1,)))
        weights, dlogits = [], []
        for k in range(SETS):
            part = slice(k * rows, (k + 1) * rows)
            logits = raw[:, part]
            if k == 0:
                logits = jnp.where(key_index <= query_index, logits, -FAR)
                norm, delta = stat_own[h, 0:1], stat_own[h, 1:2]
            else:
                hidden = jnp.where(table_ref[k - 1, c] > 0, 0.0, FAR).astype(F32)
                norm, delta = stat_in[c, k - 1, 0:1] + hidden, stat_in[c, k - 1, 1:2]
            probs = jnp.exp2(logits - norm)
            weights.append(probs.astype(BF16))
            dlogits.append((probs * (prob_grad[:, part] - delta)).astype(BF16))
        dlogit = jnp.concatenate(dlogits, axis=1)
        terms = dot(kv[0, c, 0], dlogit, ((0,), (0,))) * scale
        held[h] = terms[:, :rows]
        for k in range(1, SETS):
            term[h, k - 1] = terms[:, k * rows : (k + 1) * rows].astype(BF16)

        @pl.when(has_near)
        def _():
            term_copy(1, c, up).start()

        @pl.when(even_or_up)
        def _():
            term_copy(3, c, pair).start()

        dk_ref[:, cols(c, HDIM)] = (dot(dlogit, queries, ((1,), (0,))) * scale).astype(BF16)
        weight = jnp.concatenate(weights, axis=1)
        dv_ref[:, cols(c, HDIM)] = dot(weight, grads, ((1,), (0,))).astype(BF16)

    def merge(c):
        h = c - keyed

        @pl.when(has_both)
        def _():
            term_copy(1, c, me).wait_recv()

        @pl.when(jnp.logical_or(odd, has_up))
        def _():
            term_copy(3, c, me).wait_recv()

        @pl.when(has_up)
        def _():
            side = jnp.where(even, back[h, 2].astype(F32), 0.0)
            total = term[h, 1].astype(F32) + back[h, 0].astype(F32) + side
            term[h, 1] = total.astype(BF16)
            term_copy(2, c, up).start()

    def close(c):
        h = c - keyed

        @pl.when(has_down)
        def _():
            term_copy(2, c, me).wait_recv()

        side = jnp.where(odd, back[h, 2].astype(F32), 0.0)
        total = held[h] + back[h, 1].astype(F32) + side
        dq_ref[:, cols(c, HDIM)] = total.T.astype(BF16)

    plan = []
    for low, high, timed in (
        (
            0,
            keyed,
            (
                (side_q, -91.11, 1.92),
                (send_kv, -51.98, 9.29),
                (send_q, -2.16, 0.60),
                (relay_kv, 11.21, 6.52),
                (relay_q, 22.85, 7.09),
                (attend, 24.91, 6.64),
                (finish, 51.12, 10.08),
            ),
        ),
        (
            keyed,
            heads,
            (
                (send_q, -45.24, 38.26),
                (side_q, -7.31, 23.83),
                (relay_q, 2.36, 0.25),
                (ask, 33.73, 0.72),
                (combine, 39.90, 0.59),
                (answer, 51.27, 0.22),
                (merge, 58.78, 18.74),
                (close, 119.40, 149.97),
            ),
        ),
    ):
        for action, start, step in timed:
            for c in range(low, high):
                plan.append((start + step * (c - low), functools.partial(action, c)))

    for due, action, *where in (
        (-35.11, arrive, 2, 0),
        (-27.21, arrive, 2, 1),
        (-24.12, arrive, 3, 0),
        (-8.84, arrive, 1, 0),
        (-0.76, hand_on, 2),
        (4.43, arrive, 3, 1),
        (8.56, hand_on, 0),
        (19.32, arrive, 1, 1),
        (22.67, take, 2),
        (22.76, take, 0),
        (23.92, hand_on, 3),
        (26.91, some, 3),
        (28.55, hand_on, 1),
        (31.47, rest, 3),
        (31.58, some, 1),
        (37.51, rest, 1),
    ):
        plan.append((due, functools.partial(action, *where)))

    for t in range(heads // 2):
        plan.append((-30.0 + t * 0.001, load_proj(t).start))

    plan.sort(key=lambda entry: entry[0])
    for _, action in plan:
        action()

    def drain(present, ref, sem):
        @pl.when(present)
        def _():
            pltpu.make_async_copy(ref, ref, sem).wait()

    always = me >= 0
    odd_or_up = jnp.logical_or(odd, has_up)
    drain(always, og.at[0, :, pl.ds(0, (lanes - 1) * width)], lane_send.at[0])
    for k, kv_sent, q_sent, term_sent in (
        (1, has_both, has_both, has_near),
        (2, has_up, has_down, has_up),
        (3, jnp.logical_or(even, has_down), odd_or_up, even_or_up),
    ):
        drain(here[k], og.at[k, :, pl.ds(0, (lanes - 1) * width)], lane_send.at[k])
        drain(q_sent, og.at[0, :, pl.ds(0, width)], og_send.at[k - 1])
        drain(q_sent, qs.at[:, k], q_send.at[k - 1])
        drain(kv_sent, kv.at[:, pl.ds(0, keyed), k], kv_send.at[k - 1])
        drain(reach[k], stat_out.at[:, k - 1], stat_send.at[k - 1])
        drain(here[k], part_out.at[:, k - 1], part_send.at[k - 1])
        drain(term_sent, term.at[:, k - 1], term_send.at[k - 1])


def publish_kernel(*refs):
    number = (len(refs) - 1) // 2
    copies = [
        pltpu.make_async_copy(refs[a], refs[number + a], refs[-1].at[a]) for a in range(number)
    ]
    for copy in copies:
        copy.start()
    for copy in copies:
        copy.wait()


def publish(arrays):
    number = len(arrays)
    held = [pltpu.with_memory_space_constraint(a, pltpu.VMEM) for a in arrays]
    return pl.pallas_call(
        publish_kernel,
        out_shape=[jax.ShapeDtypeStruct(a.shape, a.dtype) for a in arrays],
        in_specs=[pl.BlockSpec(memory_space=pltpu.VMEM)] * number,
        out_specs=[pl.BlockSpec(memory_space=pl.ANY)] * number,
        scratch_shapes=[pltpu.SemaphoreType.DMA((number,))],
        compiler_params=pltpu.CompilerParams(vmem_limit_bytes=2**20),
    )(*held)


def body(count, lanes, queries, key_rows, value_rows, out_grad, out_proj, table, active):
    rows, columns = queries.shape
    heads = columns // HDIM
    smem = pl.BlockSpec(memory_space=pltpu.SMEM)
    vmem = pl.BlockSpec(memory_space=pltpu.VMEM)
    hbm = pl.BlockSpec(memory_space=pl.ANY)
    dma = pltpu.SemaphoreType.DMA
    grads = pl.pallas_call(
        functools.partial(kernel, count, lanes),
        out_shape=[pltpu.VMEM((rows, columns), BF16)] * 3,
        in_specs=[hbm] * 5 + [smem] * 2,
        out_specs=[vmem] * 3,
        scratch_shapes=[
            pltpu.VMEM((2, heads, SETS, rows, HDIM), BF16),
            pltpu.VMEM((heads, SETS, rows, HDIM), BF16),
            pltpu.VMEM((heads, SETS, rows, HDIM), BF16),
            pltpu.VMEM((SETS, rows, out_proj.shape[1]), BF16),
            pltpu.VMEM(out_proj.shape, BF16),
            pltpu.VMEM((2, heads, rows, HDIM), F32),
            pltpu.VMEM((heads, SECTIONS, 2, rows), F32),
            pltpu.VMEM((heads, SECTIONS, 2, rows), F32),
            pltpu.VMEM((ASKED, 3, rows), F32),
            pltpu.VMEM((ASKED, SECTIONS, 3, rows), F32),
            pltpu.VMEM((ASKED, SECTIONS, 3, rows), F32),
            pltpu.VMEM((ASKED, 2, rows), F32),
            pltpu.VMEM((ASKED, HDIM, rows), F32),
            pltpu.VMEM((ASKED, SECTIONS, HDIM, rows), BF16),
            pltpu.VMEM((ASKED, SECTIONS, HDIM, rows), BF16),
            dma((2, heads)),
            dma((heads,)),
            dma((1 + heads // 2,)),
            dma((SECTIONS,)),
            dma((SECTIONS, heads)),
            dma((SECTIONS,)),
            dma((SECTIONS, heads)),
            dma((SECTIONS,)),
            dma((SECTIONS, 2)),
            dma((SETS,)),
            dma((SETS, 2, lanes)),
            dma((SECTIONS,)),
            dma((SECTIONS, heads)),
            dma((SECTIONS,)),
            dma((SECTIONS, ASKED)),
            dma((SECTIONS,)),
            dma((SECTIONS, ASKED)),
        ],
        compiler_params=pltpu.CompilerParams(
            collective_id=0, has_side_effects=True, vmem_limit_bytes=60 * 2**20
        ),
    )(queries, key_rows, value_rows, out_grad, out_proj, table.T, active)
    return tuple(publish(grads))


def solution(mesh):
    return jax.shard_map(
        functools.partial(body, mesh.shape["seq"], mesh.shape["head"]),
        mesh=mesh,
        in_specs=(
            P("seq", "head"),
            P("seq", "head"),
            P("seq", "head"),
            P("seq", "head"),
            P("head", None),
            P("head", None),
            P("seq", None),
        ),
        out_specs=(P("seq", "head"), P("seq", "head"), P("seq", "head")),
        check_vma=False,
    )
```

time: 67.8 us -> 54.4 us (0.80)
  Pallas kernels: 67 us -> 53.4 us
    pallas_call x2, Pallas kernels: 67 us -> 53.4 us  [the longest x1 52.2 us: body(): pl.pallas_call(functools.partial(kernel, count, lanes), out_shape=[pltpu....]
where the time goes in v2:
time: 54.4 us; the launch traced here: 54.2 us
  Pallas kernels  53.4 us (98%)
  between operations  0.8 us (1%)
    pallas_call x1, Pallas kernels, body(): pl.pallas_call(functools.partial(kernel, count, lanes), out_shape=[pltpu....  52.2 us
    pallas_call x1, Pallas kernels, publish(): pl.pallas_call(publish_kernel, out_shape=[jax.ShapeDtypeStruct(a.shape, a...  1.17 us

profile of v2, /device:TPU:0, one launch (start us, length us, event | category | flops | bytes accessed | tf_op | source)
XLA Modules:
  0.0 54.2 jit_solution(1443255416051235951)
XLA Ops:
  0.6 52.2 %shard_map.94 = (bf16[256,1024]{1,0:T(8,128)(2,1)S(1)}, bf16[256,1024]{1,0:T(8,128)(2,1)S(1)}, bf16[256,1024]{1,0:T(8,128)(2,1)S(1)}) custom-call(bf16[256,1024]{1,0:T(8,128)(2,1)} %q_hbm.1, bf16[256,1024]{1,0:T(8,128)(2,1)} %k_hbm.1, bf16[256,1024]{1,0:T(8,128)(2,1)} %v_hbm.1, bf16[256,512]{1,0:T(8,128)(2,1)} %og_hbm.1, bf16[1024,2048]{1,0:T(8,128)(2,1)} %proj_hbm.1, ...), custom_call_target="tpu_custom_call" | custom-call | tf_op jit(solution)/shard_map/pallas_call | solution.py:720
  52.8 1.2 %shard_map.95 = (bf16[256,1024]{1,0:T(8,128)(2,1)}, bf16[256,1024]{1,0:T(8,128)(2,1)}, bf16[256,1024]{1,0:T(8,128)(2,1)}) custom-call(bf16[256,1024]{1,0:T(8,128)(2,1)S(1)} %get-tuple-element.6.refs_0_, bf16[256,1024]{1,0:T(8,128)(2,1)S(1)} %get-tuple-element.7.refs_1_, bf16[256,1024]{1,0:T(8,128)(2,1)S(1)} %get-tuple-element.8.refs_2_), custom_call_target="tpu_custom_call" | custom-call | tf_op jit(solution)/shard_map/pallas_call | solution.py:703

commit v3 on v2

--- a/solution.py
+++ b/solution.py
@@ -31,8 +31,8 @@
     v_hbm,
     og_hbm,
     proj_hbm,
-    table_ref,
-    active_ref,
+    table_hbm,
+    active_hbm,
     dq_ref,
     dk_ref,
     dv_ref,
@@ -51,8 +51,8 @@
     held,
     term,
     back,
-    kv_load,
-    q_load,
+    table_ref,
+    active_ref,
     load_sem,
     kv_send,
     kv_recv,
@@ -61,7 +61,8 @@
     og_send,
     og_recv,
     lane_send,
-    lane_recv,
+    peer_recv,
+    twin_recv,
     stat_send,
     stat_recv,
     part_send,
@@ -117,12 +118,13 @@
             target,
         )
 
-    def q_copy(k, source, c, target):
+    def q_copy(k, source, g, target):
+        duo = pl.ds(2 * g, 2)
         return remote(
-            qs.at[c, source],
-            qs.at[c, k],
+            qs.at[duo, source],
+            qs.at[duo, k],
             q_send.at[k - 1],
-            q_recv.at[k - 1, c],
+            q_recv.at[k - 1, g],
             "seq",
             target,
         )
@@ -138,18 +140,20 @@
             target,
         )
 
-    def lane_copy(k, shard, p, target):
+    def peer_copy(k, j, shard, p, target):
         part = og.at[k, pl.ds(p * piece, piece), cols(shard, width)]
+        return remote(part, part, lane_send.at[k], peer_recv.at[k, p, j], "head", target)
+
+    def twin_copy(k, shard, p):
+        part = og.at[k, pl.ds(p * piece, piece), cols(shard, width)]
+        return remote(part, part, lane_send.at[k], twin_recv.at[k], "head", twin)
+
+    def part_copy(k, target):
         return remote(
-            part, part, lane_send.at[k], lane_recv.at[k, p, shard], "head", target
-        )
-
-    def part_copy(k, c, target):
-        return remote(
-            part_out.at[c - keyed, k - 1],
-            part_in.at[c - keyed, k - 1],
+            part_out.at[:, k - 1],
+            part_in.at[:, k - 1],
             part_send.at[k - 1],
-            part_recv.at[k - 1, c - keyed],
+            part_recv.at[k - 1],
             "seq",
             target,
         )
@@ -164,23 +168,22 @@
             target,
         )
 
-    def stat_copy(k, c, target):
+    groups = [(0, keyed - 2), (keyed - 2, keyed - 1), (keyed - 1, keyed), (keyed, heads)]
+
+    def group_of(c):
+        return [low <= c < high for low, high in groups].index(True)
+
+    def stat_copy(k, group, target):
+        low, high = groups[group]
+        some_heads = pl.ds(low, high - low)
         return remote(
-            stat_out.at[c, k - 1],
-            stat_in.at[c, k - 1],
+            stat_out.at[some_heads, k - 1],
+            stat_in.at[some_heads, k - 1],
             stat_send.at[k - 1],
-            stat_recv.at[k - 1, c],
+            stat_recv.at[k - 1, group],
             "seq",
             target,
         )
-
-    def load_kv(c, j):
-        return pltpu.make_async_copy(
-            (k_hbm, v_hbm)[j].at[:, cols(c, HDIM)], kv.at[j, c, 0], kv_load.at[j, c]
-        )
-
-    def load_q(c):
-        return pltpu.make_async_copy(q_hbm.at[:, cols(c, HDIM)], qs.at[c, 0], q_load.at[c])
 
     barrier = pltpu.get_barrier_semaphore()
     arrivals = jnp.int32(2 + len(peers))
@@ -202,46 +205,37 @@
 
     load_og = pltpu.make_async_copy(og_hbm, og.at[0, :, cols(lane, width)], load_sem.at[0])
 
-    def load_proj(t):
-        part = pl.ds(t * 2 * HDIM, 2 * HDIM)
-        return pltpu.make_async_copy(proj_hbm.at[part], proj.at[part], load_sem.at[1 + t])
+    def load_kv(c):
+        for j, source in enumerate((k_hbm, v_hbm)):
+            pltpu.make_async_copy(
+                source.at[:, cols(c, HDIM)],
+                kv.at[j, c, 0],
+                load_sem.at[1 if c < EARLY else 2],
+            ).start()
 
     load_og.start()
     for c in range(EARLY):
-        for j in range(2):
-            load_kv(c, j).start()
+        load_kv(c)
 
     pl.semaphore_wait(barrier, arrivals)
 
     def gather_start(k, p):
-        for peer in peers:
-            lane_copy(k, lane, p, peer).start()
-        lane_copy(k, lane, p, twin).start()
+        for j, peer in enumerate(peers):
+            peer_copy(k, j, lane, p, peer).start()
+        twin_copy(k, lane, p).start()
 
     def gather_pass(k):
         for p in range(2):
-            for peer in peers:
-                lane_copy(k, peer, p, lane).wait_recv()
-                lane_copy(k, peer, p, twin).start()
+            for j in range(len(peers)):
+                shard = lax.rem(lane + lanes - 2 * (j + 1), lanes)
+                peer_copy(k, j, shard, p, lane).wait_recv()
+                twin_copy(k, shard, p).start()
 
     def gather_end(k):
-        for p in range(2):
-            lane_copy(k, twin, p, lane).wait_recv()
-            for j in range(len(peers)):
-                shard = lax.rem(twin + 2 * (j + 1), lanes)
-                lane_copy(k, shard, p, lane).wait_recv()
-
-    loaded = set()
-
-    def ready(c):
-        if c not in loaded:
-            loaded.add(c)
-            for copy in [load_q(c)] if c < heads else map(load_proj, range(heads // 2)):
-                copy.wait()
+        settle(og.at[k, :, pl.ds(0, lanes // 2 * width)], twin_recv.at[k]).wait()
 
     def send_kv(c):
-        for j in range(2):
-            load_kv(c, j).wait()
+        ready("early" if c < EARLY else "late")
 
         @pl.when(has_up)
         def _():
@@ -252,14 +246,14 @@
             kv_copy(3, 0, c, pair).start()
 
     def send_q(c):
-        ready(c)
+        ready("query")
 
         @pl.when(has_down)
         def _():
             q_copy(2, 0, c, down).start()
 
     def side_q(c):
-        ready(c)
+        ready("query")
 
         @pl.when(odd)
         def _():
@@ -304,11 +298,39 @@
             og_copy(3, 0, p, pair).start()
 
     for c in range(EARLY, heads):
-        for j in range(2):
-            load_kv(c, j).start()
+        load_kv(c)
 
     for c in range(heads):
-        load_q(c).start()
+        pltpu.make_async_copy(
+            q_hbm.at[:, cols(c, HDIM)], qs.at[c, 0], load_sem.at[3]
+        ).start()
+
+    tables = [
+        pltpu.make_async_copy(table_hbm, table_ref, load_sem.at[5]),
+        pltpu.make_async_copy(active_hbm, active_ref, load_sem.at[6]),
+    ]
+    for copy in tables:
+        copy.start()
+
+    def load_proj(t):
+        part = pl.ds(t * 2 * HDIM, 2 * HDIM)
+        return pltpu.make_async_copy(proj_hbm.at[part], proj.at[part], load_sem.at[4])
+
+    def settle(ref, sem):
+        return pltpu.make_async_copy(ref, ref, sem)
+
+    pending = {
+        "early": [settle(kv.at[:, pl.ds(0, EARLY), 0], load_sem.at[1])],
+        "late": [settle(kv.at[:, pl.ds(EARLY, heads - EARLY), 0], load_sem.at[2])],
+        "query": [settle(qs.at[:, 0], load_sem.at[3])],
+        "proj": [settle(proj, load_sem.at[4])],
+        "table": tables,
+    }
+
+    def ready(*names):
+        for name in names:
+            for copy in pending.pop(name, ()):
+                copy.wait()
 
     here = {0: me >= 0, 1: has_near, 2: has_up, 3: even_or_up}
     reach = {1: has_far, 2: has_down, 3: odd_or_down}
@@ -351,7 +373,7 @@
     query_index = lax.broadcasted_iota(jnp.int32, (rows, rows), 1)
 
     def attend(c):
-        ready(c)
+        ready("query", "table")
         for k in (1, 3):
 
             @pl.when(reach[k])
@@ -359,51 +381,79 @@
                 kv_copy(k, 0, c, me).wait_recv()
 
         query, grad = qs[c, 0], gs[c, 0]
-        raw = dot(kv[0, c].reshape(SETS * rows, HDIM), query, ((1,), (1,))) * scale2
-        prob_grad = dot(kv[1, c].reshape(SETS * rows, HDIM), grad, ((1,), (1,)))
-        logits = [raw[k * rows : (k + 1) * rows] for k in range(SETS)]
-        prob_grads = [prob_grad[k * rows : (k + 1) * rows] for k in range(SETS)]
-        logits[0] = jnp.where(key_index <= query_index, logits[0], -FAR)
-        top = jnp.max(logits[0], axis=0, keepdims=True)
-        usable = {}
-        for k in range(1, SETS):
-            usable[k] = jnp.logical_and(
-                table_ref[k - 1, c] * active_ref[0, k - 1] > 0, me >= count // 2**k
-            )
-            best = jnp.max(logits[k], axis=0, keepdims=True)
-            top = jnp.maximum(top, best + jnp.where(usable[k], 0.0, -FAR).astype(F32))
-        total, weighted, exps = 0.0, 0.0, []
+        tops, totals, sums, exps, prob_grads = [], [], [], [], []
         for k in range(SETS):
-            shift = top if k == 0 else top + jnp.where(usable[k], 0.0, FAR).astype(F32)
-            exps.append(jnp.exp2(logits[k] - shift))
-            total = total + jnp.sum(exps[k], axis=0, keepdims=True)
-            weighted = weighted + jnp.sum(exps[k] * prob_grads[k], axis=0, keepdims=True)
+            logits = dot(kv[0, c, k], query, ((1,), (1,))) * scale2
+            if k == 0:
+                logits = jnp.where(key_index <= query_index, logits, -FAR)
+            prob_grads.append(dot(kv[1, c, k], grad, ((1,), (1,))))
+            best = jnp.max(logits, axis=0, keepdims=True)
+            exps.append(jnp.exp2(logits - best))
+            totals.append(jnp.sum(exps[k], axis=0, keepdims=True))
+            sums.append(jnp.sum(exps[k] * prob_grads[k], axis=0, keepdims=True))
+            if k:
+                usable = jnp.logical_and(
+                    table_ref[k - 1, c] * active_ref[0, k - 1] > 0, me >= count // 2**k
+                )
+                best = best + jnp.where(usable, 0.0, -FAR).astype(F32)
+            tops.append(best)
+        top = functools.reduce(jnp.maximum, tops)
+        shares = [jnp.exp2(x - top) for x in tops]
+        total = sum(share * x for share, x in zip(shares, totals))
         inverse = 1.0 / total
-        delta = weighted * inverse
+        delta = sum(share * x for share, x in zip(shares, sums)) * inverse
         norm = top + jnp.log2(total)
         for k in range(1, SETS):
             hidden = jnp.where(active_ref[0, k - 1] > 0, 0.0, FAR).astype(F32)
             stat_out[c, k - 1] = jnp.concatenate([norm + hidden, delta], axis=0)
 
-        probs = exps[0] * inverse
+        probs = exps[0] * (shares[0] * inverse)
         dlogit = (probs * (prob_grads[0] - delta)).astype(BF16)
+        terms = dot(kv[0, c, 0], dlogit, ((0,), (0,)))
+        for k in range(1, SETS):
+            part = (exps[k] * (prob_grads[k] - delta)).astype(BF16)
+            terms = terms + dot(kv[0, c, k], part, ((0,), (0,))) * (shares[k] * inverse)
         own[0, c] = dot(dlogit, query, ((1,), (0,))) * scale
         own[1, c] = dot(probs.astype(BF16), grad, ((1,), (0,)))
-        others = jnp.concatenate(
-            [(exps[k] * (prob_grads[k] - delta)).astype(BF16) for k in range(1, SETS)], axis=0
-        )
-        keys = kv[0, c, 1:].reshape(SECTIONS * rows, HDIM)
-        far = dot(keys, others, ((0,), (0,))) * inverse
-        near = dot(kv[0, c, 0], dlogit, ((0,), (0,)))
-        dq_ref[:, cols(c, HDIM)] = ((far + near) * scale).T.astype(BF16)
+        dq_ref[:, cols(c, HDIM)] = (terms * scale).T.astype(BF16)
         tell(c)
 
     def tell(c):
+        group = group_of(c)
+        if c + 1 < groups[group][1]:
+            return
+
         for k, go, span in ((1, has_far, half), (2, has_down, quarter), (3, odd_or_down, eighth)):
 
             @pl.when(go)
             def _():
-                stat_copy(k, c, me - span).start()
+                stat_copy(k, group, me - span).start()
+
+    heard = set()
+
+    def hear(group):
+        if group in heard:
+            return
+
+        heard.add(group)
+        for k, span in ((1, half), (2, quarter), (3, eighth)):
+
+            @pl.when(here[k])
+            def _():
+                stat_copy(k, group, me + span).wait_recv()
+
+    asked_for = set()
+
+    def meet(g):
+        if g in asked_for:
+            return
+
+        asked_for.add(g)
+        for k in (1, 3):
+
+            @pl.when(here[k])
+            def _():
+                q_copy(k, 0, g, me).wait_recv()
 
     def collect(c):
         queries = qs[c, 1:].reshape(SECTIONS * rows, HDIM)
@@ -423,18 +473,8 @@
         dv_ref[:, cols(c, HDIM)] = (own[1, c] + value).astype(BF16)
 
     def finish(c):
-        for k, source in ((1, half), (2, quarter), (3, eighth)):
-
-            @pl.when(here[k])
-            def _():
-                stat_copy(k, c, me + source).wait_recv()
-
-        for k in (1, 3):
-
-            @pl.when(here[k])
-            def _():
-                q_copy(k, 0, c, me).wait_recv()
-
+        hear(group_of(c))
+        meet(c // 2)
         collect(c)
 
     def arrive(k, p):
@@ -459,7 +499,7 @@
             gather_pass(k)
 
     def take(k, low=0, high=heads):
-        ready(heads)
+        ready("proj")
 
         @pl.when(here[k])
         def _():
@@ -474,15 +514,22 @@
         def _():
             project(k, 0, keyed)
 
-    def ask(c):
-        for k in (1, 3):
+    def ask(first):
+        ready("late", "table")
+        for c in range(first, heads):
+            if c % 2 == 0:
+                meet(c // 2)
+
+        for c in range(first, heads):
+            ask_one(c)
+
+        for k, span in ((1, half), (2, quarter), (3, eighth)):
 
             @pl.when(here[k])
             def _():
-                q_copy(k, 0, c, me).wait_recv()
-
-        for j in range(2):
-            load_kv(c, j).wait()
+                part_copy(k, me + span).start()
+
+    def ask_one(c):
         raw = dot(kv[0, c, 0], qs[c].reshape(SETS * rows, HDIM), ((1,), (1,))) * scale2
         prob_grad = dot(kv[1, c, 0], gs[c].reshape(SETS * rows, HDIM), ((1,), (1,)))
         for k in range(SETS):
@@ -499,19 +546,19 @@
             else:
                 top = top + jnp.where(table_ref[k - 1, c] > 0, 0.0, -FAR).astype(F32)
                 part_out[c - keyed, k - 1] = jnp.concatenate([top, total, weighted], axis=0)
-        for k, span in ((1, half), (2, quarter), (3, eighth)):
-
-            @pl.when(here[k])
-            def _():
-                part_copy(k, c, me + span).start()
-
-    def combine(c):
+    def combine(first):
         for k in range(1, SETS):
 
             @pl.when(reach[k])
             def _():
-                part_copy(k, c, me).wait_recv()
-
+                part_copy(k, me).wait_recv()
+
+        for c in range(first, heads):
+            combine_one(c)
+
+        tell(heads - 1)
+
+    def combine_one(c):
         h = c - keyed
         tops, parts = [part_own[h, 0:1]], [(part_own[h, 1:2], part_own[h, 2:3])]
         for k in range(1, SETS):
@@ -529,15 +576,9 @@
         for k in range(1, SETS):
             hidden = jnp.where(active_ref[0, k - 1] > 0, 0.0, FAR).astype(F32)
             stat_out[c, k - 1] = jnp.concatenate([norm + hidden, delta], axis=0)
-        tell(c)
 
     def answer(c):
-        for k, span in ((1, half), (2, quarter), (3, eighth)):
-
-            @pl.when(here[k])
-            def _():
-                stat_copy(k, c, me + span).wait_recv()
-
+        hear(group_of(c))
         h = c - keyed
         queries = qs[c].reshape(SETS * rows, HDIM)
         grads = gs[c].reshape(SETS * rows, HDIM)
@@ -609,27 +650,37 @@
             0,
             keyed,
             (
-                (side_q, -91.11, 1.92),
-                (send_kv, -51.98, 9.29),
-                (send_q, -2.16, 0.60),
-                (relay_kv, 11.21, 6.52),
-                (relay_q, 22.85, 7.09),
-                (attend, 24.91, 6.64),
-                (finish, 51.12, 10.08),
+                (send_kv, -35.51, 6.09),
+                (relay_kv, -26.96, 13.35),
+                (attend, 20.51, 7.47),
+                (finish, 60.00, 14.65),
+            ),
+        ),
+        (
+            0,
+            keyed // 2,
+            (
+                (side_q, -35.62, 5.18),
+                (send_q, -20.83, 16.78),
+                (relay_q, 16.85, 10.96),
+            ),
+        ),
+        (
+            keyed // 2,
+            heads // 2,
+            (
+                (side_q, -45.00, 2.05),
+                (send_q, -27.91, 178.66),
+                (relay_q, -14.36, 42700.55),
             ),
         ),
         (
             keyed,
             heads,
             (
-                (send_q, -45.24, 38.26),
-                (side_q, -7.31, 23.83),
-                (relay_q, 2.36, 0.25),
-                (ask, 33.73, 0.72),
-                (combine, 39.90, 0.59),
-                (answer, 51.27, 0.22),
-                (merge, 58.78, 18.74),
-                (close, 119.40, 149.97),
+                (answer, 57.25, 0.32),
+                (merge, 60.00, 25.48),
+                (close, 119.40, 2041502.52),
             ),
         ),
     ):
@@ -638,27 +689,29 @@
                 plan.append((start + step * (c - low), functools.partial(action, c)))
 
     for due, action, *where in (
-        (-35.11, arrive, 2, 0),
-        (-27.21, arrive, 2, 1),
-        (-24.12, arrive, 3, 0),
-        (-8.84, arrive, 1, 0),
-        (-0.76, hand_on, 2),
-        (4.43, arrive, 3, 1),
-        (8.56, hand_on, 0),
-        (19.32, arrive, 1, 1),
-        (22.67, take, 2),
-        (22.76, take, 0),
-        (23.92, hand_on, 3),
-        (26.91, some, 3),
-        (28.55, hand_on, 1),
-        (31.47, rest, 3),
-        (31.58, some, 1),
-        (37.51, rest, 1),
+        (-27.93, arrive, 2, 0),
+        (-24.44, arrive, 2, 1),
+        (-20.90, hand_on, 0),
+        (-16.89, arrive, 3, 0),
+        (-10.96, hand_on, 2),
+        (-5.70, arrive, 3, 1),
+        (-1.75, take, 0),
+        (3.61, take, 2),
+        (10.57, arrive, 1, 0),
+        (14.73, arrive, 1, 1),
+        (17.89, hand_on, 3),
+        (19.08, some, 3),
+        (19.29, rest, 3),
+        (21.27, hand_on, 1),
+        (24.07, some, 1),
+        (26.23, ask, keyed),
+        (36.68, rest, 1),
+        (37.92, combine, keyed),
     ):
         plan.append((due, functools.partial(action, *where)))
 
     for t in range(heads // 2):
-        plan.append((-30.0 + t * 0.001, load_proj(t).start))
+        plan.append((-27.924 + t * 0.001, load_proj(t).start))
 
     plan.sort(key=lambda entry: entry[0])
     for _, action in plan:
@@ -667,7 +720,7 @@
     def drain(present, ref, sem):
         @pl.when(present)
         def _():
-            pltpu.make_async_copy(ref, ref, sem).wait()
+            settle(ref, sem).wait()
 
     always = me >= 0
     odd_or_up = jnp.logical_or(odd, has_up)
@@ -713,14 +766,13 @@
 def body(count, lanes, queries, key_rows, value_rows, out_grad, out_proj, table, active):
     rows, columns = queries.shape
     heads = columns // HDIM
-    smem = pl.BlockSpec(memory_space=pltpu.SMEM)
     vmem = pl.BlockSpec(memory_space=pltpu.VMEM)
     hbm = pl.BlockSpec(memory_space=pl.ANY)
     dma = pltpu.SemaphoreType.DMA
     grads = pl.pallas_call(
         functools.partial(kernel, count, lanes),
         out_shape=[pltpu.VMEM((rows, columns), BF16)] * 3,
-        in_specs=[hbm] * 5 + [smem] * 2,
+        in_specs=[hbm] * 7,
         out_specs=[vmem] * 3,
         scratch_shapes=[
             pltpu.VMEM((2, heads, SETS, rows, HDIM), BF16),
@@ -738,21 +790,22 @@
             pltpu.VMEM((ASKED, HDIM, rows), F32),
             pltpu.VMEM((ASKED, SECTIONS, HDIM, rows), BF16),
             pltpu.VMEM((ASKED, SECTIONS, HDIM, rows), BF16),
-            dma((2, heads)),
-            dma((heads,)),
-            dma((1 + heads // 2,)),
+            pltpu.SMEM((SECTIONS, heads), jnp.int32),
+            pltpu.SMEM((1, SECTIONS), jnp.int32),
+            dma((7,)),
             dma((SECTIONS,)),
-            dma((SECTIONS, heads)),
+            dma((SECTIONS, heads - ASKED)),
             dma((SECTIONS,)),
-            dma((SECTIONS, heads)),
+            dma((SECTIONS, heads // 2)),
             dma((SECTIONS,)),
             dma((SECTIONS, 2)),
             dma((SETS,)),
-            dma((SETS, 2, lanes)),
+            dma((SETS, 2, max(1, lanes // 2 - 1))),
+            dma((SETS,)),
             dma((SECTIONS,)),
-            dma((SECTIONS, heads)),
+            dma((SECTIONS, 4)),
             dma((SECTIONS,)),
-            dma((SECTIONS, ASKED)),
+            dma((SECTIONS,)),
             dma((SECTIONS,)),
             dma((SECTIONS, ASKED)),
         ],

time: 54.4 us -> 51.4 us (0.945)
  Pallas kernels: 53.4 us -> 50.4 us
    pallas_call x1, Pallas kernels: 52.2 us -> 49.2 us  [body(): pl.pallas_call(functools.partial(kernel, count, lanes), out_shape=[pltpu....]
where the time goes in v3:
time: 51.4 us; the launch traced here: 51.2 us
  Pallas kernels  50.4 us (98%)
  between operations  0.8 us (2%)
    pallas_call x1, Pallas kernels, body(): pl.pallas_call(functools.partial(kernel, count, lanes), out_shape=[pltpu....  49.2 us
    pallas_call x1, Pallas kernels, publish(): pl.pallas_call(publish_kernel, out_shape=[jax.ShapeDtypeStruct(a.shape, a...  1.17 us

profile of v3, /device:TPU:0, one launch (start us, length us, event | category | flops | bytes accessed | tf_op | source)
XLA Modules:
  0.0 51.2 jit_solution(2574577072823056048)
XLA Ops:
  0.6 49.2 %shard_map.94 = (bf16[256,1024]{1,0:T(8,128)(2,1)S(1)}, bf16[256,1024]{1,0:T(8,128)(2,1)S(1)}, bf16[256,1024]{1,0:T(8,128)(2,1)S(1)}) custom-call(bf16[256,1024]{1,0:T(8,128)(2,1)} %q_hbm.1, bf16[256,1024]{1,0:T(8,128)(2,1)} %k_hbm.1, bf16[256,1024]{1,0:T(8,128)(2,1)} %v_hbm.1, bf16[256,512]{1,0:T(8,128)(2,1)} %og_hbm.1, bf16[1024,2048]{1,0:T(8,128)(2,1)} %proj_hbm.1, ...), custom_call_target="tpu_custom_call" | custom-call | tf_op jit(solution)/shard_map/pallas_call | solution.py:772
  49.9 1.2 %shard_map.95 = (bf16[256,1024]{1,0:T(8,128)(2,1)}, bf16[256,1024]{1,0:T(8,128)(2,1)}, bf16[256,1024]{1,0:T(8,128)(2,1)}) custom-call(bf16[256,1024]{1,0:T(8,128)(2,1)S(1)} %get-tuple-element.6.refs_0_, bf16[256,1024]{1,0:T(8,128)(2,1)S(1)} %get-tuple-element.7.refs_1_, bf16[256,1024]{1,0:T(8,128)(2,1)S(1)} %get-tuple-element.8.refs_2_), custom_call_target="tpu_custom_call" | custom-call | tf_op jit(solution)/shard_map/pallas_call | solution.py:756

commit v4 on v3

--- a/solution.py
+++ b/solution.py
@@ -285,33 +285,10 @@
         def _():
             q_copy(3, 2, c, pair).start()
 
-    load_og.wait()
-    for p in range(2):
-        gather_start(0, p)
-
-        @pl.when(has_down)
-        def _():
-            og_copy(2, 0, p, down).start()
-
-        @pl.when(odd)
-        def _():
-            og_copy(3, 0, p, pair).start()
-
-    for c in range(EARLY, heads):
-        load_kv(c)
-
-    for c in range(heads):
-        pltpu.make_async_copy(
-            q_hbm.at[:, cols(c, HDIM)], qs.at[c, 0], load_sem.at[3]
-        ).start()
-
     tables = [
         pltpu.make_async_copy(table_hbm, table_ref, load_sem.at[5]),
         pltpu.make_async_copy(active_hbm, active_ref, load_sem.at[6]),
     ]
-    for copy in tables:
-        copy.start()
-
     def load_proj(t):
         part = pl.ds(t * 2 * HDIM, 2 * HDIM)
         return pltpu.make_async_copy(proj_hbm.at[part], proj.at[part], load_sem.at[4])
@@ -334,32 +311,62 @@
 
     here = {0: me >= 0, 1: has_near, 2: has_up, 3: even_or_up}
     reach = {1: has_far, 2: has_down, 3: odd_or_down}
-    for k in range(1, SETS):
-
-        @pl.when(jnp.logical_not(reach[k]))
-        def _():
-            @pl.loop(0, keyed)
-            def _(c):
-                for j in range(2):
-                    kv[j, c, k] = jnp.zeros((rows, HDIM), BF16)
-
-            for c in range(ASKED):
-                part_in[c, k - 1] = jnp.full((3, rows), -FAR, F32)
-
-        @pl.when(jnp.logical_not(here[k]))
-        def _():
-            @pl.loop(0, heads)
-            def _(c):
-                qs[c, k] = jnp.zeros((rows, HDIM), BF16)
-                gs[c, k] = jnp.zeros((rows, HDIM), BF16)
-                stat_in[c, k - 1] = jnp.full((2, rows), FAR, F32)
-
-    for k, present in ((1, has_both), (2, has_down), (3, jnp.logical_or(odd, has_up))):
-
-        @pl.when(jnp.logical_not(present))
-        def _():
-            for c in range(ASKED):
-                back[c, k - 1] = jnp.zeros((HDIM, rows), BF16)
+    def fetch():
+        for c in range(EARLY, heads):
+            load_kv(c)
+
+        for c in range(heads):
+            pltpu.make_async_copy(
+                q_hbm.at[:, cols(c, HDIM)], qs.at[c, 0], load_sem.at[3]
+            ).start()
+
+        for copy in tables:
+            copy.start()
+
+    def clear():
+        for k in range(1, SETS):
+
+            @pl.when(jnp.logical_not(reach[k]))
+            def _():
+                @pl.loop(0, keyed)
+                def _(c):
+                    for j in range(2):
+                        kv[j, c, k] = jnp.zeros((rows, HDIM), BF16)
+
+                for c in range(ASKED):
+                    part_in[c, k - 1] = jnp.full((3, rows), -FAR, F32)
+
+            @pl.when(jnp.logical_not(here[k]))
+            def _():
+                @pl.loop(0, heads)
+                def _(c):
+                    qs[c, k] = jnp.zeros((rows, HDIM), BF16)
+                    gs[c, k] = jnp.zeros((rows, HDIM), BF16)
+                    stat_in[c, k - 1] = jnp.full((2, rows), FAR, F32)
+
+        for k, present in ((1, has_both), (2, has_down), (3, jnp.logical_or(odd, has_up))):
+
+            @pl.when(jnp.logical_not(present))
+            def _():
+                for c in range(ASKED):
+                    back[c, k - 1] = jnp.zeros((HDIM, rows), BF16)
+
+    load_og.wait()
+    for p in range(2):
+        gather_start(0, p)
+
+        @pl.when(has_down)
+        def _():
+            og_copy(2, 0, p, down).start()
+
+        @pl.when(odd)
+        def _():
+            og_copy(3, 0, p, pair).start()
+
+    for c in range(EARLY):
+        send_kv(c)
+
+    fetch()
 
     def project(k, low, high):
         @pl.loop(low // 2, high // 2)
@@ -646,11 +653,11 @@
 
     plan = []
     for low, high, timed in (
+        (EARLY, keyed, ((send_kv, -23.33, 6.09),)),
         (
             0,
             keyed,
             (
-                (send_kv, -35.51, 6.09),
                 (relay_kv, -26.96, 13.35),
                 (attend, 20.51, 7.47),
                 (finish, 60.00, 14.65),
@@ -713,6 +720,7 @@
     for t in range(heads // 2):
         plan.append((-27.924 + t * 0.001, load_proj(t).start))
 
+    plan.append((-27.918, clear))
     plan.sort(key=lambda entry: entry[0])
     for _, action in plan:
         action()

time: 51.4 us -> 49.7 us (0.967)
  Pallas kernels: 50.4 us -> 48.7 us
    pallas_call x1, Pallas kernels: 49.2 us -> 47.5 us  [body(): pl.pallas_call(functools.partial(kernel, count, lanes), out_shape=[pltpu....]
where the time goes in v4:
time: 49.7 us; the launch traced here: 49.5 us
  Pallas kernels  48.7 us (98%)
  between operations  0.8 us (2%)
    pallas_call x1, Pallas kernels, body(): pl.pallas_call(functools.partial(kernel, count, lanes), out_shape=[pltpu....  47.5 us
    pallas_call x1, Pallas kernels, publish(): pl.pallas_call(publish_kernel, out_shape=[jax.ShapeDtypeStruct(a.shape, a...  1.17 us

profile of v4, /device:TPU:0, one launch (start us, length us, event | category | flops | bytes accessed | tf_op | source)
XLA Modules:
  0.0 49.5 jit_solution(6442329877750517481)
XLA Ops:
  0.6 47.5 %shard_map.94 = (bf16[256,1024]{1,0:T(8,128)(2,1)S(1)}, bf16[256,1024]{1,0:T(8,128)(2,1)S(1)}, bf16[256,1024]{1,0:T(8,128)(2,1)S(1)}) custom-call(bf16[256,1024]{1,0:T(8,128)(2,1)} %q_hbm.1, bf16[256,1024]{1,0:T(8,128)(2,1)} %k_hbm.1, bf16[256,1024]{1,0:T(8,128)(2,1)} %v_hbm.1, bf16[256,512]{1,0:T(8,128)(2,1)} %og_hbm.1, bf16[1024,2048]{1,0:T(8,128)(2,1)} %proj_hbm.1, ...), custom_call_target="tpu_custom_call" | custom-call | tf_op jit(solution)/shard_map/pallas_call | solution.py:780
  48.2 1.2 %shard_map.95 = (bf16[256,1024]{1,0:T(8,128)(2,1)}, bf16[256,1024]{1,0:T(8,128)(2,1)}, bf16[256,1024]{1,0:T(8,128)(2,1)}) custom-call(bf16[256,1024]{1,0:T(8,128)(2,1)S(1)} %get-tuple-element.6.refs_0_, bf16[256,1024]{1,0:T(8,128)(2,1)S(1)} %get-tuple-element.7.refs_1_, bf16[256,1024]{1,0:T(8,128)(2,1)S(1)} %get-tuple-element.8.refs_2_), custom_call_target="tpu_custom_call" | custom-call | tf_op jit(solution)/shard_map/pallas_call | solution.py:764

commit v5 on v4

--- a/solution.py
+++ b/solution.py
@@ -369,8 +369,7 @@
     fetch()
 
     def project(k, low, high):
-        @pl.loop(low // 2, high // 2)
-        def _(t):
+        for t in range(low // 2, high // 2):
             tile = proj[cols(t, 2 * HDIM), :]
             grad = dot(og[k], tile, ((1,), (1,))).astype(BF16)
             gs[2 * t, k] = grad[:, :HDIM]
@@ -660,16 +659,16 @@
             (
                 (relay_kv, -26.96, 13.35),
                 (attend, 20.51, 7.47),
-                (finish, 60.00, 14.65),
+                (finish, 60.00, 11.97),
             ),
         ),
         (
             0,
             keyed // 2,
             (
-                (side_q, -35.62, 5.18),
-                (send_q, -20.83, 16.78),
-                (relay_q, 16.85, 10.96),
+                (side_q, -35.62, 6.80),
+                (send_q, -20.90, 13.31),
+                (relay_q, 16.37, 10.96),
             ),
         ),
         (
@@ -677,8 +676,8 @@
             heads // 2,
             (
                 (side_q, -45.00, 2.05),
-                (send_q, -27.91, 178.66),
-                (relay_q, -14.36, 42700.55),
+                (send_q, -34.11, 178.66),
+                (relay_q, -14.51, 42700.55),
             ),
         ),
         (
@@ -698,21 +697,21 @@
     for due, action, *where in (
         (-27.93, arrive, 2, 0),
         (-24.44, arrive, 2, 1),
-        (-20.90, hand_on, 0),
-        (-16.89, arrive, 3, 0),
-        (-10.96, hand_on, 2),
+        (-23.63, hand_on, 0),
+        (-17.30, arrive, 3, 0),
+        (-10.64, hand_on, 2),
+        (-5.73, take, 0),
         (-5.70, arrive, 3, 1),
-        (-1.75, take, 0),
-        (3.61, take, 2),
+        (4.22, take, 2),
         (10.57, arrive, 1, 0),
         (14.73, arrive, 1, 1),
-        (17.89, hand_on, 3),
+        (17.82, hand_on, 3),
         (19.08, some, 3),
-        (19.29, rest, 3),
+        (20.89, rest, 3),
         (21.27, hand_on, 1),
         (24.07, some, 1),
         (26.23, ask, keyed),
-        (36.68, rest, 1),
+        (36.01, rest, 1),
         (37.92, combine, keyed),
     ):
         plan.append((due, functools.partial(action, *where)))

time: 49.7 us -> 49.4 us (level)
  no operation moved by 1% of the time
where the time goes in v5:
time: 49.4 us; the launch traced here: 49.2 us
  Pallas kernels  48.4 us (98%)
  between operations  0.8 us (2%)
    pallas_call x1, Pallas kernels, body(): pl.pallas_call(functools.partial(kernel, count, lanes), out_shape=[pltpu....  47.2 us
    pallas_call x1, Pallas kernels, publish(): pl.pallas_call(publish_kernel, out_shape=[jax.ShapeDtypeStruct(a.shape, a...  1.17 us

profile of v5, /device:TPU:0, one launch (start us, length us, event | category | flops | bytes accessed | tf_op | source)
XLA Modules:
  0.0 49.2 jit_solution(9661691324633305461)
XLA Ops:
  0.6 47.2 %shard_map.94 = (bf16[256,1024]{1,0:T(8,128)(2,1)S(1)}, bf16[256,1024]{1,0:T(8,128)(2,1)S(1)}, bf16[256,1024]{1,0:T(8,128)(2,1)S(1)}) custom-call(bf16[256,1024]{1,0:T(8,128)(2,1)} %q_hbm.1, bf16[256,1024]{1,0:T(8,128)(2,1)} %k_hbm.1, bf16[256,1024]{1,0:T(8,128)(2,1)} %v_hbm.1, bf16[256,512]{1,0:T(8,128)(2,1)} %og_hbm.1, bf16[1024,2048]{1,0:T(8,128)(2,1)} %proj_hbm.1, ...), custom_call_target="tpu_custom_call" | custom-call | tf_op jit(solution)/shard_map/pallas_call | solution.py:779
  47.8 1.2 %shard_map.95 = (bf16[256,1024]{1,0:T(8,128)(2,1)}, bf16[256,1024]{1,0:T(8,128)(2,1)}, bf16[256,1024]{1,0:T(8,128)(2,1)}) custom-call(bf16[256,1024]{1,0:T(8,128)(2,1)S(1)} %get-tuple-element.6.refs_0_, bf16[256,1024]{1,0:T(8,128)(2,1)S(1)} %get-tuple-element.7.refs_1_, bf16[256,1024]{1,0:T(8,128)(2,1)S(1)} %get-tuple-element.8.refs_2_), custom_call_target="tpu_custom_call" | custom-call | tf_op jit(solution)/shard_map/pallas_call | solution.py:763
